TPU v7x, 32 devices: a whole 2x2x4 slice. The times are simulated.
32 devices in a mesh: row: 2 (over x), col: 4 (over y, core), depth: 4 (over z).
Axes of the slice: x: 2, y: 2, z: 4, core: 2. Of those that a mesh axis runs over, the one named last changes fastest.
Arguments:
- left_values: bfloat16 [96, 32, 4, 529], P('row', ('col', 'depth')), may hold values from -1.25 to 1.25
- left_columns: int32 [96, 32, 4], P('row', ('col', 'depth')), may hold values from 0 to 39, as said below
- right_values: bfloat16 [32, 40, 4, 3, 529], P(('col', 'depth'), 'row'), may hold values from -1.75 to 1.75
- right_columns: int32 [32, 40, 4, 3], P(('col', 'depth'), 'row'), may hold values from 0 to 31, as said below
Outputs:
- product_matrix: bfloat16 [2208, 2944], P('row', ('col', 'depth'))
Inputs may be any that keep to these rules, and one draw needn't show every extreme that they name: `left_columns`: within one block row and panel the 4 entries are distinct. `right_columns`: within one block row and column tile the 3 entries are distinct.
All inputs are finite; a program needn't handle non-finite values.
Results may differ from a plain program's by a relative error of at most 0.001.
Values may be sent and summed in bfloat16 or wider, within the bound.
A program may use at most 192 MiB of HBM per device.

v0:
```python
import functools
import math

import jax
import jax.numpy as jnp
from jax import lax
from jax.experimental import pallas as pl
from jax.experimental.pallas import tpu as pltpu
from jax.sharding import PartitionSpec as P

CTW = 32


def lay_left(values, columns):
    rows, panels, slots, square = values.shape
    edge = math.isqrt(square)
    blocks = values.reshape(rows, panels, slots, edge, edge).transpose(1, 2, 4, 0, 3)
    blocks = blocks.reshape(panels, slots, edge, rows * edge)
    codes = jnp.repeat(columns.transpose(1, 2, 0).astype(jnp.bfloat16), edge, axis=2)
    return jnp.concatenate([blocks, codes[:, :, None, :]], axis=2)


def lay_right(values, columns):
    panels, rows, tiles, slots, square = values.shape
    edge = math.isqrt(square)
    blocks = values.reshape(panels, rows, tiles, slots, edge, edge).transpose(2, 0, 3, 5, 1, 4)
    blocks = jnp.pad(blocks, ((0, 0),) * 5 + ((0, 1),))
    blocks = blocks.reshape(tiles, panels, slots, edge, rows * (edge + 1))
    codes = jnp.repeat(columns.transpose(2, 0, 3, 1).astype(jnp.bfloat16), edge + 1, axis=3)
    return jnp.concatenate([blocks, codes[:, :, :, None, :]], axis=3)


def expand(values_ref, lead, slots, pad, count, out_ref, base):
    width = out_ref.shape[-1]
    lower = lax.broadcasted_iota(jnp.int32, (2 * pad, width), 0) >= pad
    shift = jnp.where(lower, 1.0, 0.0)
    doubled, codes = [], []
    for s in range(slots):
        one = values_ref[lead + (s,)].astype(jnp.float32)
        code = jnp.broadcast_to(one[pad - 1 : pad, :], (2 * pad, width)) - shift
        doubled.append(jnp.concatenate([one, one], axis=0).astype(jnp.bfloat16))
        codes.append(code.astype(jnp.bfloat16))
    for pair in range(count // 2):
        want = jnp.bfloat16(base + 2 * pair)
        filled = jnp.zeros((2 * pad, width), jnp.bfloat16)
        for s in range(slots):
            filled = jnp.where(codes[s] == want, doubled[s], filled)
        out_ref[2 * pad * pair : 2 * pad * (pair + 1), :] = filled


def product_kernel(pad, left_ref, right_ref, out_ref, left_dense, right_dense):
    @pl.when(pl.program_id(0) == 0)
    def _():
        out_ref[...] = jnp.zeros_like(out_ref)

    parts, _, slots_r = right_ref.shape[:3]
    slots_l = left_ref.shape[1]
    here = left_dense.shape[1] // pad
    for r in range(parts):
        expand(left_ref, (0,), slots_l, pad, here, left_dense.at[r], r * here)
        expand(right_ref, (r, 0), slots_r, pad, CTW, right_dense.at[r], 0)
    total = out_ref[...]
    for r in range(parts):
        total += jnp.dot(right_dense[r], left_dense[r], preferred_element_type=jnp.float32)
    out_ref[...] = total


def product(left, right, pad):
    panels, slots_l, _, m = left.shape
    parts, _, slots_r, _, k = right.shape
    n = CTW * pad
    return pl.pallas_call(
        functools.partial(product_kernel, pad),
        grid=(panels,),
        in_specs=[
            pl.BlockSpec((1, slots_l, pad, m), lambda p: (p, 0, 0, 0)),
            pl.BlockSpec((parts, 1, slots_r, pad, k), lambda p: (0, p, 0, 0, 0)),
        ],
        out_specs=pl.BlockSpec((n, m), lambda p: (0, 0)),
        out_shape=jax.ShapeDtypeStruct((n, m), jnp.float32),
        scratch_shapes=[pltpu.VMEM((parts, k, m), jnp.bfloat16), pltpu.VMEM((parts, n, k), jnp.bfloat16)],
        compiler_params=pltpu.CompilerParams(vmem_limit_bytes=56 << 20),
    )(left, right)


def gather_kernel(columns, rows, left_ref, right_ref, left_out, right_out, left_send, left_recv, tile_send, tile_recv, row_send, row_recv):
    me_col, me_row = lax.axis_index("col"), lax.axis_index("row")
    mesh_id = pl.DeviceIdType.MESH
    barrier = pltpu.get_barrier_semaphore()
    for d in range(1, columns):
        pl.semaphore_signal(barrier, inc=1, device_id={"col": lax.rem(me_col + d, columns)}, device_id_type=mesh_id)
    for d in range(1, rows):
        pl.semaphore_signal(barrier, inc=1, device_id={"row": lax.rem(me_row + d, rows)}, device_id_type=mesh_id)
    pl.semaphore_wait(barrier, columns + rows - 2)

    tile_hops, left_hops, row_hops = [], [], []
    for d in range(1, columns):
        other = lax.rem(me_col + d, columns)
        tile_hops.append(
            pltpu.make_async_remote_copy(
                src_ref=right_ref.at[other],
                dst_ref=right_out.at[me_row, me_col],
                send_sem=tile_send.at[d],
                recv_sem=tile_recv.at[d],
                device_id={"col": other},
                device_id_type=mesh_id,
            )
        )

    paired = columns % 2 == 0
    partner = me_col + 1 - 2 * lax.rem(me_col, 2)

    def left_hop(i, source, slot, other):
        return pltpu.make_async_remote_copy(
            src_ref=source,
            dst_ref=left_out.at[slot],
            send_sem=left_send.at[i],
            recv_sem=left_recv.at[i],
            device_id={"col": other},
            device_id_type=mesh_id,
        )

    strides = range(2, columns, 2) if paired else range(1, columns)
    left_hops = [left_hop(d, left_ref, me_col, lax.rem(me_col + d, columns)) for d in strides]
    passed = [left_hop(1, left_ref, me_col, partner)] if paired else []

    def to_rows(d, source):
        slot = lax.rem(me_col + columns - d, columns)
        for e in range(1, rows):
            hop = pltpu.make_async_remote_copy(
                src_ref=source,
                dst_ref=right_out.at[me_row, slot],
                send_sem=row_send.at[e, d],
                recv_sem=row_recv.at[e, d],
                device_id={"row": lax.rem(me_row + e, rows)},
                device_id_type=mesh_id,
            )
            hop.start()
            row_hops.append(hop)

    for hop in tile_hops:
        hop.start()
    to_rows(0, right_ref.at[me_col])
    for hop in left_hops + passed:
        hop.start()
    left_out[me_col] = left_ref[...]
    right_out[me_row, me_col] = right_ref[me_col]
    for d, hop in enumerate(tile_hops, 1):
        hop.wait_recv()
        to_rows(d, right_out.at[me_row, lax.rem(me_col + columns - d, columns)])
    for d, hop in zip(strides, left_hops):
        hop.wait_recv()
        if paired:
            slot = lax.rem(me_col + columns - d, columns)
            passed.append(left_hop(d + 1, left_out.at[slot], slot, partner))
            passed[-1].start()
    for hop in passed + row_hops:
        hop.wait_recv()
    for hop in tile_hops + left_hops + passed + row_hops:
        hop.wait_send()


def gather(left, right, columns, rows):
    whole = pl.BlockSpec(memory_space=pltpu.VMEM)
    dma = pltpu.SemaphoreType.DMA
    return pl.pallas_call(
        functools.partial(gather_kernel, columns, rows),
        in_specs=[whole, whole],
        out_specs=[whole, whole],
        out_shape=[
            jax.ShapeDtypeStruct((columns,) + left.shape, left.dtype),
            jax.ShapeDtypeStruct((rows,) + right.shape, right.dtype),
        ],
        scratch_shapes=[dma((columns,))] * 4 + [dma((rows, columns))] * 2,
        compiler_params=pltpu.CompilerParams(collective_id=1, has_side_effects=True, vmem_limit_bytes=32 << 20),
    )(left, right)


def ring_kernel(streams, own_ref, out_ref, landed, send_sem, recv_sem):
    n = own_ref.shape[0]
    me = lax.axis_index("depth")
    after, before = lax.rem(me + 1, n), lax.rem(me + n - 1, n)
    barrier = pltpu.get_barrier_semaphore()
    for other in (before, after):
        pl.semaphore_signal(barrier, inc=1, device_id={"depth": other}, device_id_type=pl.DeviceIdType.MESH)
    pl.semaphore_wait(barrier, 2)

    rows = own_ref.shape[1] // streams
    spans = [pl.ds(rows * i, rows) for i in range(streams)]

    def hop(step, i, source):
        return pltpu.make_async_remote_copy(
            src_ref=source,
            dst_ref=landed.at[step, spans[i]],
            send_sem=send_sem.at[step, i],
            recv_sem=recv_sem.at[step, i],
            device_id={"depth": before if i % 2 else after},
            device_id_type=pl.DeviceIdType.MESH,
        )

    def chunk(step, i):
        return lax.rem(me + 1 + step, n) if i % 2 else lax.rem(me + 2 * n - 1 - step, n)

    hops = {}
    for i in range(streams):
        hops[0, i] = hop(0, i, own_ref.at[chunk(0, i), spans[i]])
        hops[0, i].start()
    for step in range(n - 1):
        for i in range(streams):
            hops[step, i].wait_recv()
            total = landed[step, spans[i], :] + own_ref[chunk(step + 1, i), spans[i], :]
            if step == n - 2:
                out_ref[spans[i], :] = total
            else:
                landed[step, spans[i], :] = total
                hops[step + 1, i] = hop(step + 1, i, landed.at[step, spans[i]])
                hops[step + 1, i].start()
    for each in hops.values():
        each.wait_send()


def ring_sum(partial_sums, n):
    rows, m = partial_sums.shape[0] // n, partial_sums.shape[1]
    streams = 4
    whole = pl.BlockSpec(memory_space=pltpu.VMEM)
    return pl.pallas_call(
        functools.partial(ring_kernel, streams),
        in_specs=[whole],
        out_specs=whole,
        out_shape=jax.ShapeDtypeStruct((rows, m), jnp.float32),
        scratch_shapes=[
            pltpu.VMEM((n - 1, rows, m), jnp.float32),
            pltpu.SemaphoreType.DMA((n - 1, streams)),
            pltpu.SemaphoreType.DMA((n - 1, streams)),
        ],
        compiler_params=pltpu.CompilerParams(collective_id=0, has_side_effects=True, vmem_limit_bytes=32 << 20),
    )(partial_sums.reshape(n, rows, m))


def body(columns, rows, depth, left_values, left_columns, right_values, right_columns):
    pad = math.isqrt(left_values.shape[-1]) + 1
    left, right = gather(
        lay_left(left_values, left_columns), lay_right(right_values, right_columns), columns, rows
    )
    left = left.reshape((-1,) + left.shape[2:])
    right = right.reshape((rows, -1) + right.shape[3:])
    if right_values.shape[1] % 2:
        right = right.transpose(1, 2, 3, 0, 4)
        right = right.reshape((1,) + right.shape[:3] + (-1,))
    partial_sums = product(left, right, pad)
    result = ring_sum(partial_sums, depth)
    kept, m = result.shape
    result = result.reshape(kept // pad, pad, m)[:, : pad - 1].reshape(kept // pad * (pad - 1), m)
    return result.T.astype(jnp.bfloat16)


def solution(mesh):
    placed = (
        P("row", ("col", "depth"), None, None),
        P("row", ("col", "depth"), None),
        P(("col", "depth"), "row", None, None, None),
        P(("col", "depth"), "row", None, None),
    )
    return jax.shard_map(
        functools.partial(body, mesh.shape["col"], mesh.shape["row"], mesh.shape["depth"]), mesh=mesh, in_specs=placed, out_specs=P("row", ("col", "depth")), check_vma=False
    )
```

profile of v0, /device:TPU:8, one launch (start us, length us, event | category | flops | bytes accessed | tf_op | source)
XLA Modules:
  0.0 137.2 jit_solution(16092279467042511470)
XLA Ops:
  0.0 4.9 %reshape.29 = bf16[2,20,4,3,23,23]{5,4,2,3,1,0:T(8,128)(2,1)} reshape(bf16[2,20,4,3,529]{4,2,3,1,0:T(4,128)(2,1)} %param.6) | data formatting | bytes 1015680 | tf_op jit(solution)/shard_map/reshape | solution.py:26
  4.9 6.3 %copy.14 = bf16[4,2,3,23,20,23]{5,4,3,2,1,0:T(8,128)(2,1)S(1)} copy(bf16[4,2,3,23,20,23]{3,5,0,2,4,1:T(8,128)(2,1)} %bitcast.25) | data formatting | bytes 1015680
  11.2 2.5 %pad.4.clone = bf16[4,2,3,23,20,24]{5,4,3,2,1,0:T(8,128)(2,1)} pad(bf16[4,2,3,23,20,23]{5,4,3,2,1,0:T(8,128)(2,1)S(1)} %copy.14, bf16[]{:T(256)} %constant.2.clone.1), padding=0_0x0_0x0_0x0_0x0_0x0_1 | pad | bytes 1037762 | tf_op jit(solution)/shard_map/jit(_pad)/pad | solution.py:27
  13.7 0.0 copy-start.4
  13.7 4.3 %reshape.30 = bf16[4,2,3,23,480]{4,3,2,1,0:T(8,128)(2,1)S(1)} reshape(bf16[4,2,3,23,20,24]{5,4,3,2,1,0:T(8,128)(2,1)} %pad.4.clone) | data formatting | bytes 1059840 | tf_op jit(solution)/shard_map/reshape | solution.py:28
  18.0 0.0 copy-done.4
  18.0 0.0 copy-start.3
  18.0 0.1 broadcast_in_dim.7
  18.2 0.2 broadcast_in_dim_reshape.7
  18.4 0.2 pad_maximum_fusion.right_ref
  18.6 0.5 copy-done.3
  19.0 2.1 %copy.8 = bf16[48,2,4,529]{0,2,3,1:T(4,128)(2,1)} copy(bf16[48,2,4,529]{3,2,1,0:T(4,128)(2,1)S(1)} %copy-done.3) | data formatting | bytes 812544 | tf_op args[0]
  21.2 3.4 %copy.9 = bf16[2,4,23,48,23]{4,3,2,1,0:T(8,128)(2,1)S(1)} copy(bf16[2,4,23,48,23]{3,1,2,4,0:T(4,128)(2,1)} %bitcast.26) | data formatting | bytes 812544 | tf_op jit(solution)/shard_map/transpose | solution.py:17
  24.5 0.0 copy-start.5
  24.6 2.4 %reshape.28 = bf16[2,4,23,1104]{3,2,1,0:T(8,128)(2,1)S(1)} reshape(bf16[2,4,23,48,23]{4,3,2,1,0:T(8,128)(2,1)S(1)} %copy.9) | data formatting | bytes 812544 | tf_op jit(solution)/shard_map/reshape | solution.py:18
  27.0 0.0 copy-done.5
  27.0 0.1 broadcast_in_dim.6
  27.1 0.2 broadcast_in_dim_reshape.8
  27.3 0.1 pad_maximum_fusion.1.left_ref
  27.4 21.0 %shard_map.46 = (bf16[4,2,4,24,1104]{4,3,2,1,0:T(8,128)(2,1)S(1)}, bf16[2,4,2,3,24,480]{5,4,3,2,1,0:T(8,128)(2,1)S(1)}) custom-call(bf16[2,4,24,1104]{3,2,1,0:T(8,128)(2,1)S(1)} %pad_maximum_fusion.1.left_ref, bf16[4,2,3,24,480]{4,3,2,1,0:T(8,128)(2,1)S(1)} %pad_maximum_fusion.right_ref), custom_call_target="tpu_custom_call" | custom-call | tf_op jit(solution)/shard_map/pallas_call | solution.py:166
  48.4 0.0 copy-start.1
  48.4 1.2 copy-done.1
  49.6 0.0 copy-start.2
  49.6 1.1 copy-done.2
  50.7 22.4 %shard_map.47 = f32[768,1104]{1,0:T(8,128)} custom-call(bf16[8,4,24,1104]{3,2,1,0:T(8,128)(2,1)} %bitcast.23, bf16[2,8,3,24,480]{4,3,2,1,0:T(8,128)(2,1)} %bitcast.24), custom_call_target="tpu_custom_call" | custom-call | tf_op jit(solution)/shard_map/pallas_call | solution.py:72
  73.1 0.0 copy-start
  73.1 2.0 %copy-done = f32[768,1104]{1,0:T(8,128)S(1)} copy-done((f32[768,1104]{1,0:T(8,128)S(1)}, f32[768,1104]{1,0:T(8,128)}, u32[]{:S(2)}) %copy-start) | copy-done | bytes 3391512
  75.1 61.1 %shard_map.48 = f32[192,1104]{1,0:T(8,128)S(1)} custom-call(f32[4,192,1104]{2,1,0:T(8,128)S(1)} %bitcast.22), custom_call_target="tpu_custom_call" | custom-call | tf_op jit(solution)/shard_map/pallas_call | solution.py:226
  136.2 0.1 convert.4
  136.3 0.9 convert_element_type.25
  (4 shorter events, 0.1 us)
Async XLA Ops:
  13.7 4.3 %copy-start.4 = (s32[2,20,4,3]{1,2,3,0:T(4,128)S(1)}, s32[2,20,4,3]{1,2,3,0:T(4,128)}, u32[]{:S(2)}) copy-start(s32[2,20,4,3]{1,2,3,0:T(4,128)} %param.7) | copy-start | bytes 5764
  18.0 1.0 copy-start.3
  24.5 2.4 %copy-start.5 = (s32[48,2,4]{0,2,1:T(4,128)S(1)}, s32[48,2,4]{0,2,1:T(4,128)}, u32[]{:S(2)}) copy-start(s32[48,2,4]{0,2,1:T(4,128)} %param.5) | copy-start | bytes 4612
  48.4 1.2 copy-start.1
  49.6 1.1 copy-start.2
  73.1 2.0 %copy-start = (f32[768,1104]{1,0:T(8,128)S(1)}, f32[768,1104]{1,0:T(8,128)}, u32[]{:S(2)}) copy-start(f32[768,1104]{1,0:T(8,128)} %shard_map.47) | copy-start | bytes 10174468
where the time goes:
time: 139 us; the launch traced here: 137 us
  Pallas kernels  105 us (76%)
  local copies, waits for them, and re-layouts  32.2 us (23%)
    pallas_call x1, Pallas kernels, ring_sum(): pl.pallas_call(functools.partial(ring_kernel, streams), in_specs=[whole],...  61.1 us
    pallas_call x1, Pallas kernels, product(): pl.pallas_call(functools.partial(product_kernel, pad), grid=(panels,), in...  22.4 us
    pallas_call x1, Pallas kernels, gather(): pl.pallas_call(functools.partial(gather_kernel, columns, rows), in_specs=...  21 us
    unnamed x14, local copies, waits for them, and re-layouts  13.2 us
    reshape x1, local copies, waits for them, and re-layouts, lay_right(): values.reshape(panels, rows, tiles, slots, edge, edge)  4.91 us
    reshape x1, local copies, waits for them, and re-layouts, lay_right(): blocks = blocks.reshape(tiles, panels, slots, edge, rows * (edge + 1))  4.3 us
    transpose x1, local copies, waits for them, and re-layouts, lay_left(): values.reshape(rows, panels, slots, edge, edge).transpose(1, 2, 4, 0, 3)  3.37 us

commit v1 on v0

--- a/solution.py
+++ b/solution.py
@@ -48,38 +48,185 @@
         out_ref[2 * pad * pair : 2 * pad * (pair + 1), :] = filled
 
 
-def product_kernel(pad, left_ref, right_ref, out_ref, left_dense, right_dense):
-    @pl.when(pl.program_id(0) == 0)
+FULL = 32700.0
+
+
+def encode(x, pad):
+    row = lax.broadcasted_iota(jnp.int32, x.shape, 0)
+    x = jnp.where(row % pad == pad - 1, 0.0, x)
+    most = jnp.maximum(jnp.max(jnp.abs(x), axis=0, keepdims=True), 1e-30)
+    power = jnp.floor(jnp.log2(most)) + 1.0
+    coded = jnp.round(x * (jnp.exp2(-power) * FULL))
+    return jnp.where(row == pad - 1, power, coded).astype(jnp.int32).astype(jnp.int16)
+
+
+def decode(coded, pad):
+    x = coded.astype(jnp.int32).astype(jnp.float32)
+    return x * (jnp.exp2(x[pad - 1 : pad, :]) * (1.0 / FULL))
+
+
+def reduce_kernel(pad, n, piece, left_ref, right_ref, out_ref, left_dense, right_dense, sums, r_out, r_in, l_out, l_in, r_send, r_recv, l_send, l_recv):
+    me = lax.axis_index("depth")
+    mesh_id = pl.DeviceIdType.MESH
+    barrier = pltpu.get_barrier_semaphore()
+
+    @pl.when(me > 0)
     def _():
-        out_ref[...] = jnp.zeros_like(out_ref)
-
-    parts, _, slots_r = right_ref.shape[:3]
+        pl.semaphore_signal(barrier, inc=1, device_id={"depth": me - 1}, device_id_type=mesh_id)
+
+    @pl.when(me < n - 1)
+    def _():
+        pl.semaphore_signal(barrier, inc=1, device_id={"depth": me + 1}, device_id_type=mesh_id)
+
+    pl.semaphore_wait(barrier, jnp.where(me > 0, 1, 0) + jnp.where(me < n - 1, 1, 0))
+
+    parts, panels, slots_r = right_ref.shape[:3]
     slots_l = left_ref.shape[1]
-    here = left_dense.shape[1] // pad
-    for r in range(parts):
-        expand(left_ref, (0,), slots_l, pad, here, left_dense.at[r], r * here)
-        expand(right_ref, (r, 0), slots_r, pad, CTW, right_dense.at[r], 0)
-    total = out_ref[...]
-    for r in range(parts):
-        total += jnp.dot(right_dense[r], left_dense[r], preferred_element_type=jnp.float32)
-    out_ref[...] = total
-
-
-def product(left, right, pad):
+    here = left_dense.shape[2] // pad
+    rows = sums.shape[1]
+    per = rows // pad
+    pieces = rows // piece
+
+    def span(i):
+        return pl.ds(pl.multiple_of(i * piece, piece), piece)
+
+    def right_hop(t, i):
+        return pltpu.make_async_remote_copy(
+            src_ref=r_out.at[t, span(i)], dst_ref=r_in.at[t, span(i)],
+            send_sem=r_send.at[t, i], recv_sem=r_recv.at[t, i],
+            device_id={"depth": me + 1}, device_id_type=mesh_id,
+        )
+
+    def left_hop(t, i):
+        return pltpu.make_async_remote_copy(
+            src_ref=l_out.at[t, span(i)], dst_ref=l_in.at[t, span(i)],
+            send_sem=l_send.at[t, i], recv_sem=l_recv.at[t, i],
+            device_id={"depth": me - 1}, device_id_type=mesh_id,
+        )
+
+    def fill_left(p, carry):
+        for r in range(parts):
+            expand(left_ref, (p,), slots_l, pad, here, left_dense.at[p, r], r * here)
+        return carry
+
+    lax.fori_loop(0, panels, fill_left, 0)
+
+    after, before = n - 1 - me, me
+    lead = jnp.where(after >= before, after - before, before - after)
+    near = jnp.where(after >= before, before, after)
+
+    def chunk_step(step, carry):
+        s = step - lead
+        distance = near - s // 2
+        paired = jnp.where(s % 2 == 0, me + distance, me - distance)
+        alone = jnp.where(after >= before, n - 1 - step, step)
+        d = jnp.where(step < lead, alone, paired)
+        base = d * per
+
+        def fill_right(p, inner):
+            for r in range(parts):
+                expand(right_ref, (r, p), slots_r, pad, per, right_dense.at[p, r], base)
+            return inner
+
+        lax.fori_loop(0, panels, fill_right, 0)
+        sums[d] = jnp.zeros(sums.shape[1:], jnp.float32)
+
+        def add(p, inner):
+            total = sums[d]
+            for r in range(parts):
+                total += jnp.dot(right_dense[p, r], left_dense[p, r], preferred_element_type=jnp.float32)
+            sums[d] = total
+            return inner
+
+        lax.fori_loop(0, panels, add, 0)
+
+        @pl.when((me == 0) & (d > 0))
+        def _():
+            def send(i, inner):
+                r_out[n - 1 - d, span(i), :] = encode(sums[d, span(i), :], pad)
+                right_hop(n - 1 - d, i).start()
+                return inner
+
+            lax.fori_loop(0, pieces, send, 0)
+
+        @pl.when((me == n - 1) & (d < n - 1))
+        def _():
+            def send(i, inner):
+                l_out[d, span(i), :] = encode(sums[d, span(i), :], pad)
+                left_hop(d, i).start()
+                return inner
+
+            lax.fori_loop(0, pieces, send, 0)
+
+        return carry
+
+    lax.fori_loop(0, n, chunk_step, 0)
+
+    def pass_on(step, carry):
+        t, i = step // pieces, step % pieces
+        d = n - 1 - t
+
+        @pl.when((me > 0) & (me <= d))
+        def _():
+            right_hop(t, i).wait_recv()
+            sums[d, span(i), :] += decode(r_in[t, span(i), :], pad)
+
+        @pl.when((me > 0) & (me < d))
+        def _():
+            r_out[t, span(i), :] = encode(sums[d, span(i), :], pad)
+            right_hop(t, i).start()
+
+        @pl.when((me < n - 1) & (me >= t))
+        def _():
+            left_hop(t, i).wait_recv()
+            sums[t, span(i), :] += decode(l_in[t, span(i), :], pad)
+
+        @pl.when((me < n - 1) & (me > t))
+        def _():
+            l_out[t, span(i), :] = encode(sums[t, span(i), :], pad)
+            left_hop(t, i).start()
+
+        return carry
+
+    lax.fori_loop(0, (n - 1) * pieces, pass_on, 0)
+    out_ref[...] = sums[me]
+
+    def drain(step, carry):
+        t, i = step // pieces, step % pieces
+
+        @pl.when(me < n - 1 - t)
+        def _():
+            right_hop(t, i).wait_send()
+
+        @pl.when(me > t)
+        def _():
+            left_hop(t, i).wait_send()
+
+        return carry
+
+    lax.fori_loop(0, (n - 1) * pieces, drain, 0)
+
+
+def product(left, right, pad, n):
     panels, slots_l, _, m = left.shape
     parts, _, slots_r, _, k = right.shape
-    n = CTW * pad
+    rows = CTW // n * pad
+    piece = 2 * pad
+    pieces = rows // piece
+    whole = pl.BlockSpec(memory_space=pltpu.VMEM)
+    travel = pltpu.VMEM((n - 1, rows, m), jnp.int16)
+    dma = pltpu.SemaphoreType.DMA
     return pl.pallas_call(
-        functools.partial(product_kernel, pad),
-        grid=(panels,),
-        in_specs=[
-            pl.BlockSpec((1, slots_l, pad, m), lambda p: (p, 0, 0, 0)),
-            pl.BlockSpec((parts, 1, slots_r, pad, k), lambda p: (0, p, 0, 0, 0)),
-        ],
-        out_specs=pl.BlockSpec((n, m), lambda p: (0, 0)),
-        out_shape=jax.ShapeDtypeStruct((n, m), jnp.float32),
-        scratch_shapes=[pltpu.VMEM((parts, k, m), jnp.bfloat16), pltpu.VMEM((parts, n, k), jnp.bfloat16)],
-        compiler_params=pltpu.CompilerParams(vmem_limit_bytes=56 << 20),
+        functools.partial(reduce_kernel, pad, n, piece),
+        in_specs=[whole, whole],
+        out_specs=whole,
+        out_shape=jax.ShapeDtypeStruct((rows, m), jnp.float32),
+        scratch_shapes=[
+            pltpu.VMEM((panels, parts, k, m), jnp.bfloat16),
+            pltpu.VMEM((panels, parts, rows, k), jnp.bfloat16),
+            pltpu.VMEM((n, rows, m), jnp.float32),
+        ] + [travel] * 4 + [dma((n - 1, pieces))] * 4,
+        compiler_params=pltpu.CompilerParams(collective_id=0, has_side_effects=True, vmem_limit_bytes=56 << 20),
     )(left, right)
 
 
@@ -176,67 +323,6 @@
     )(left, right)
 
 
-def ring_kernel(streams, own_ref, out_ref, landed, send_sem, recv_sem):
-    n = own_ref.shape[0]
-    me = lax.axis_index("depth")
-    after, before = lax.rem(me + 1, n), lax.rem(me + n - 1, n)
-    barrier = pltpu.get_barrier_semaphore()
-    for other in (before, after):
-        pl.semaphore_signal(barrier, inc=1, device_id={"depth": other}, device_id_type=pl.DeviceIdType.MESH)
-    pl.semaphore_wait(barrier, 2)
-
-    rows = own_ref.shape[1] // streams
-    spans = [pl.ds(rows * i, rows) for i in range(streams)]
-
-    def hop(step, i, source):
-        return pltpu.make_async_remote_copy(
-            src_ref=source,
-            dst_ref=landed.at[step, spans[i]],
-            send_sem=send_sem.at[step, i],
-            recv_sem=recv_sem.at[step, i],
-            device_id={"depth": before if i % 2 else after},
-            device_id_type=pl.DeviceIdType.MESH,
-        )
-
-    def chunk(step, i):
-        return lax.rem(me + 1 + step, n) if i % 2 else lax.rem(me + 2 * n - 1 - step, n)
-
-    hops = {}
-    for i in range(streams):
-        hops[0, i] = hop(0, i, own_ref.at[chunk(0, i), spans[i]])
-        hops[0, i].start()
-    for step in range(n - 1):
-        for i in range(streams):
-            hops[step, i].wait_recv()
-            total = landed[step, spans[i], :] + own_ref[chunk(step + 1, i), spans[i], :]
-            if step == n - 2:
-                out_ref[spans[i], :] = total
-            else:
-                landed[step, spans[i], :] = total
-                hops[step + 1, i] = hop(step + 1, i, landed.at[step, spans[i]])
-                hops[step + 1, i].start()
-    for each in hops.values():
-        each.wait_send()
-
-
-def ring_sum(partial_sums, n):
-    rows, m = partial_sums.shape[0] // n, partial_sums.shape[1]
-    streams = 4
-    whole = pl.BlockSpec(memory_space=pltpu.VMEM)
-    return pl.pallas_call(
-        functools.partial(ring_kernel, streams),
-        in_specs=[whole],
-        out_specs=whole,
-        out_shape=jax.ShapeDtypeStruct((rows, m), jnp.float32),
-        scratch_shapes=[
-            pltpu.VMEM((n - 1, rows, m), jnp.float32),
-            pltpu.SemaphoreType.DMA((n - 1, streams)),
-            pltpu.SemaphoreType.DMA((n - 1, streams)),
-        ],
-        compiler_params=pltpu.CompilerParams(collective_id=0, has_side_effects=True, vmem_limit_bytes=32 << 20),
-    )(partial_sums.reshape(n, rows, m))
-
-
 def body(columns, rows, depth, left_values, left_columns, right_values, right_columns):
     pad = math.isqrt(left_values.shape[-1]) + 1
     left, right = gather(
@@ -247,8 +333,7 @@
     if right_values.shape[1] % 2:
         right = right.transpose(1, 2, 3, 0, 4)
         right = right.reshape((1,) + right.shape[:3] + (-1,))
-    partial_sums = product(left, right, pad)
-    result = ring_sum(partial_sums, depth)
+    result = product(left, right, pad, depth)
     kept, m = result.shape
     result = result.reshape(kept // pad, pad, m)[:, : pad - 1].reshape(kept // pad * (pad - 1), m)
     return result.T.astype(jnp.bfloat16)

time: 139 us -> 157 us (1.13)
  Pallas kernels: 105 us -> 125 us
  local copies, waits for them, and re-layouts: 32.2 us -> 30.2 us
    pallas_call x2 -> x1, Pallas kernels: 83.6 us -> 104 us  [product(): pl.pallas_call(functools.partial(reduce_kernel, pad, n, piece), in_specs=...]
    unnamed x14 -> x12, local copies, waits for them, and re-layouts: 13.2 us -> 11.2 us
where the time goes in v1:
time: 157 us
  Pallas kernels  125 us (80%)
  local copies, waits for them, and re-layouts  30.2 us (19%)
    pallas_call x1, Pallas kernels, product(): pl.pallas_call(functools.partial(reduce_kernel, pad, n, piece), in_specs=...  104 us
    pallas_call x1, Pallas kernels, gather(): pl.pallas_call(functools.partial(gather_kernel, columns, rows), in_specs=...  21 us
    unnamed x12, local copies, waits for them, and re-layouts  11.2 us
    reshape x1, local copies, waits for them, and re-layouts, lay_right(): values.reshape(panels, rows, tiles, slots, edge, edge)  4.92 us
    reshape x1, local copies, waits for them, and re-layouts, lay_right(): blocks = blocks.reshape(tiles, panels, slots, edge, rows * (edge + 1))  4.3 us
    transpose x1, local copies, waits for them, and re-layouts, lay_left(): values.reshape(rows, panels, slots, edge, edge).transpose(1, 2, 4, 0, 3)  3.37 us

profile of v1, /device:TPU:8, one launch (start us, length us, event | category | flops | bytes accessed | tf_op | source)
XLA Modules:
  0.0 156.6 jit_solution(685531257974818668)
XLA Ops:
  0.0 4.9 %reshape.26 = bf16[2,20,4,3,23,23]{5,4,2,3,1,0:T(8,128)(2,1)} reshape(bf16[2,20,4,3,529]{4,2,3,1,0:T(4,128)(2,1)} %param.6) | data formatting | bytes 1015680 | tf_op jit(solution)/shard_map/reshape | solution.py:26
  4.9 6.3 %copy.14 = bf16[4,2,3,23,20,23]{5,4,3,2,1,0:T(8,128)(2,1)S(1)} copy(bf16[4,2,3,23,20,23]{3,5,0,2,4,1:T(8,128)(2,1)} %bitcast.23) | data formatting | bytes 1015680
  11.2 2.5 %pad.4.clone = bf16[4,2,3,23,20,24]{5,4,3,2,1,0:T(8,128)(2,1)} pad(bf16[4,2,3,23,20,23]{5,4,3,2,1,0:T(8,128)(2,1)S(1)} %copy.14, bf16[]{:T(256)} %constant.2.clone.1), padding=0_0x0_0x0_0x0_0x0_0x0_1 | pad | bytes 1037762 | tf_op jit(solution)/shard_map/jit(_pad)/pad | solution.py:27
  13.7 0.0 copy-start.3
  13.7 4.3 %reshape.27 = bf16[4,2,3,23,480]{4,3,2,1,0:T(8,128)(2,1)S(1)} reshape(bf16[4,2,3,23,20,24]{5,4,3,2,1,0:T(8,128)(2,1)} %pad.4.clone) | data formatting | bytes 1059840 | tf_op jit(solution)/shard_map/reshape | solution.py:28
  18.0 0.0 copy-done.3
  18.0 0.0 copy-start.2
  18.1 0.1 broadcast_in_dim.7
  18.2 0.2 broadcast_in_dim_reshape.7
  18.4 0.2 pad_maximum_fusion.right_ref
  18.6 0.5 copy-done.2
  19.0 2.1 %copy.8 = bf16[48,2,4,529]{0,2,3,1:T(4,128)(2,1)} copy(bf16[48,2,4,529]{3,2,1,0:T(4,128)(2,1)S(1)} %copy-done.2) | data formatting | bytes 812544 | tf_op args[0]
  21.2 3.4 %copy.9 = bf16[2,4,23,48,23]{4,3,2,1,0:T(8,128)(2,1)S(1)} copy(bf16[2,4,23,48,23]{3,1,2,4,0:T(4,128)(2,1)} %bitcast.24) | data formatting | bytes 812544 | tf_op jit(solution)/shard_map/transpose | solution.py:17
  24.5 0.0 copy-start.4
  24.6 2.4 %reshape.25 = bf16[2,4,23,1104]{3,2,1,0:T(8,128)(2,1)S(1)} reshape(bf16[2,4,23,48,23]{4,3,2,1,0:T(8,128)(2,1)S(1)} %copy.9) | data formatting | bytes 812544 | tf_op jit(solution)/shard_map/reshape | solution.py:18
  27.0 0.0 copy-done.4
  27.0 0.1 broadcast_in_dim.6
  27.1 0.2 broadcast_in_dim_reshape.8
  27.3 0.1 pad_maximum_fusion.1.left_ref
  27.4 21.0 %shard_map.46 = (bf16[4,2,4,24,1104]{4,3,2,1,0:T(8,128)(2,1)S(1)}, bf16[2,4,2,3,24,480]{5,4,3,2,1,0:T(8,128)(2,1)S(1)}) custom-call(bf16[2,4,24,1104]{3,2,1,0:T(8,128)(2,1)S(1)} %pad_maximum_fusion.1.left_ref, bf16[4,2,3,24,480]{4,3,2,1,0:T(8,128)(2,1)S(1)} %pad_maximum_fusion.right_ref), custom_call_target="tpu_custom_call" | custom-call | tf_op jit(solution)/shard_map/pallas_call | solution.py:313
  48.4 0.0 copy-start
  48.4 1.2 copy-done
  49.6 0.0 copy-start.1
  49.6 1.0 copy-done.1
  50.6 103.8 %shard_map.47 = f32[192,1104]{1,0:T(8,128)} custom-call(bf16[8,4,24,1104]{3,2,1,0:T(8,128)(2,1)} %bitcast.21, bf16[2,8,3,24,480]{4,3,2,1,0:T(8,128)(2,1)} %bitcast.22), custom_call_target="tpu_custom_call" | custom-call | tf_op jit(solution)/shard_map/pallas_call | solution.py:219
  154.4 1.2 convert.4
  155.6 0.9 convert_element_type.25
  (4 shorter events, 0.1 us)
Async XLA Ops:
  13.7 4.3 %copy-start.3 = (s32[2,20,4,3]{1,2,3,0:T(4,128)S(1)}, s32[2,20,4,3]{1,2,3,0:T(4,128)}, u32[]{:S(2)}) copy-start(s32[2,20,4,3]{1,2,3,0:T(4,128)} %param.7) | copy-start | bytes 5764
  18.0 1.0 copy-start.2
  24.5 2.4 %copy-start.4 = (s32[48,2,4]{0,2,1:T(4,128)S(1)}, s32[48,2,4]{0,2,1:T(4,128)}, u32[]{:S(2)}) copy-start(s32[48,2,4]{0,2,1:T(4,128)} %param.5) | copy-start | bytes 4612
  48.4 1.2 copy-start
  49.6 1.0 copy-start.1

commit v2 on v1

--- a/solution.py
+++ b/solution.py
@@ -162,33 +162,40 @@
 
     lax.fori_loop(0, n, chunk_step, 0)
 
+    total = (n - 1) * pieces
+    lag = 2
+
     def pass_on(step, carry):
-        t, i = step // pieces, step % pieces
+        q = step - lag * me
+        t, i = q // pieces, q % pieces
         d = n - 1 - t
 
-        @pl.when((me > 0) & (me <= d))
+        @pl.when((q >= 0) & (q < total) & (me > 0) & (me <= d))
         def _():
             right_hop(t, i).wait_recv()
             sums[d, span(i), :] += decode(r_in[t, span(i), :], pad)
 
-        @pl.when((me > 0) & (me < d))
-        def _():
-            r_out[t, span(i), :] = encode(sums[d, span(i), :], pad)
-            right_hop(t, i).start()
-
-        @pl.when((me < n - 1) & (me >= t))
-        def _():
-            left_hop(t, i).wait_recv()
-            sums[t, span(i), :] += decode(l_in[t, span(i), :], pad)
-
-        @pl.when((me < n - 1) & (me > t))
-        def _():
-            l_out[t, span(i), :] = encode(sums[t, span(i), :], pad)
-            left_hop(t, i).start()
+            @pl.when(me < d)
+            def _():
+                r_out[t, span(i), :] = encode(sums[d, span(i), :], pad)
+                right_hop(t, i).start()
+
+        k = step - lag * (n - 1 - me)
+        u, j = k // pieces, k % pieces
+
+        @pl.when((k >= 0) & (k < total) & (me < n - 1) & (me >= u))
+        def _():
+            left_hop(u, j).wait_recv()
+            sums[u, span(j), :] += decode(l_in[u, span(j), :], pad)
+
+            @pl.when(me > u)
+            def _():
+                l_out[u, span(j), :] = encode(sums[u, span(j), :], pad)
+                left_hop(u, j).start()
 
         return carry
 
-    lax.fori_loop(0, (n - 1) * pieces, pass_on, 0)
+    lax.fori_loop(0, total + lag * (n - 1), pass_on, 0)
     out_ref[...] = sums[me]
 
     def drain(step, carry):
@@ -204,7 +211,7 @@
 
         return carry
 
-    lax.fori_loop(0, (n - 1) * pieces, drain, 0)
+    lax.fori_loop(0, total, drain, 0)
 
 
 def product(left, right, pad, n):

time: 157 us -> 114 us (0.73)
  Pallas kernels: 125 us -> 81.4 us
    pallas_call x1, Pallas kernels: 104 us -> 60.4 us  [product(): pl.pallas_call(functools.partial(reduce_kernel, pad, n, piece), in_specs=...]
where the time goes in v2:
time: 114 us; the launch traced here: 113 us
  Pallas kernels  81.4 us (71%)
  local copies, waits for them, and re-layouts  30.2 us (26%)
  other arithmetic  1.47 us (1%)
    pallas_call x1, Pallas kernels, product(): pl.pallas_call(functools.partial(reduce_kernel, pad, n, piece), in_specs=...  60.4 us
    pallas_call x1, Pallas kernels, gather(): pl.pallas_call(functools.partial(gather_kernel, columns, rows), in_specs=...  21 us
    unnamed x12, local copies, waits for them, and re-layouts  11.2 us
    reshape x1, local copies, waits for them, and re-layouts, lay_right(): values.reshape(panels, rows, tiles, slots, edge, edge)  4.92 us
    reshape x1, local copies, waits for them, and re-layouts, lay_right(): blocks = blocks.reshape(tiles, panels, slots, edge, rows * (edge + 1))  4.3 us
    transpose x1, local copies, waits for them, and re-layouts, lay_left(): values.reshape(rows, panels, slots, edge, edge).transpose(1, 2, 4, 0, 3)  3.37 us
    pad x1, local copies, waits for them, and re-layouts, lay_right(): blocks = jnp.pad(blocks, ((0, 0),) * 5 + ((0, 1),))  2.46 us
    reshape x1, local copies, waits for them, and re-layouts, lay_left(): blocks = blocks.reshape(panels, slots, edge, rows * edge)  2.41 us

profile of v2, /device:TPU:8, one launch (start us, length us, event | category | flops | bytes accessed | tf_op | source)
XLA Modules:
  0.0 113.2 jit_solution(2557294997587794561)
XLA Ops:
  0.0 4.9 %reshape.26 = bf16[2,20,4,3,23,23]{5,4,2,3,1,0:T(8,128)(2,1)} reshape(bf16[2,20,4,3,529]{4,2,3,1,0:T(4,128)(2,1)} %param.6) | data formatting | bytes 1015680 | tf_op jit(solution)/shard_map/reshape | solution.py:26
  4.9 6.3 %copy.14 = bf16[4,2,3,23,20,23]{5,4,3,2,1,0:T(8,128)(2,1)S(1)} copy(bf16[4,2,3,23,20,23]{3,5,0,2,4,1:T(8,128)(2,1)} %bitcast.23) | data formatting | bytes 1015680
  11.2 2.5 %pad.4.clone = bf16[4,2,3,23,20,24]{5,4,3,2,1,0:T(8,128)(2,1)} pad(bf16[4,2,3,23,20,23]{5,4,3,2,1,0:T(8,128)(2,1)S(1)} %copy.14, bf16[]{:T(256)} %constant.2.clone.1), padding=0_0x0_0x0_0x0_0x0_0x0_1 | pad | bytes 1037762 | tf_op jit(solution)/shard_map/jit(_pad)/pad | solution.py:27
  13.7 0.0 copy-start.3
  13.7 4.3 %reshape.27 = bf16[4,2,3,23,480]{4,3,2,1,0:T(8,128)(2,1)S(1)} reshape(bf16[4,2,3,23,20,24]{5,4,3,2,1,0:T(8,128)(2,1)} %pad.4.clone) | data formatting | bytes 1059840 | tf_op jit(solution)/shard_map/reshape | solution.py:28
  18.0 0.0 copy-done.3
  18.0 0.0 copy-start.2
  18.1 0.1 broadcast_in_dim.7
  18.2 0.2 broadcast_in_dim_reshape.7
  18.4 0.2 pad_maximum_fusion.right_ref
  18.6 0.5 copy-done.2
  19.0 2.1 %copy.8 = bf16[48,2,4,529]{0,2,3,1:T(4,128)(2,1)} copy(bf16[48,2,4,529]{3,2,1,0:T(4,128)(2,1)S(1)} %copy-done.2) | data formatting | bytes 812544 | tf_op args[0]
  21.2 3.4 %copy.9 = bf16[2,4,23,48,23]{4,3,2,1,0:T(8,128)(2,1)S(1)} copy(bf16[2,4,23,48,23]{3,1,2,4,0:T(4,128)(2,1)} %bitcast.24) | data formatting | bytes 812544 | tf_op jit(solution)/shard_map/transpose | solution.py:17
  24.5 0.0 copy-start.4
  24.6 2.4 %reshape.25 = bf16[2,4,23,1104]{3,2,1,0:T(8,128)(2,1)S(1)} reshape(bf16[2,4,23,48,23]{4,3,2,1,0:T(8,128)(2,1)S(1)} %copy.9) | data formatting | bytes 812544 | tf_op jit(solution)/shard_map/reshape | solution.py:18
  27.0 0.0 copy-done.4
  27.0 0.1 broadcast_in_dim.6
  27.1 0.2 broadcast_in_dim_reshape.8
  27.3 0.1 pad_maximum_fusion.1.left_ref
  27.4 21.0 %shard_map.46 = (bf16[4,2,4,24,1104]{4,3,2,1,0:T(8,128)(2,1)S(1)}, bf16[2,4,2,3,24,480]{5,4,3,2,1,0:T(8,128)(2,1)S(1)}) custom-call(bf16[2,4,24,1104]{3,2,1,0:T(8,128)(2,1)S(1)} %pad_maximum_fusion.1.left_ref, bf16[4,2,3,24,480]{4,3,2,1,0:T(8,128)(2,1)S(1)} %pad_maximum_fusion.right_ref), custom_call_target="tpu_custom_call" | custom-call | tf_op jit(solution)/shard_map/pallas_call | solution.py:320
  48.4 0.0 copy-start
  48.4 1.2 %copy-done = bf16[4,2,4,24,1104]{4,3,2,1,0:T(8,128)(2,1)} copy-done((bf16[4,2,4,24,1104]{4,3,2,1,0:T(8,128)(2,1)}, bf16[4,2,4,24,1104]{4,3,2,1,0:T(8,128)(2,1)S(1)}, u32[]{:S(2)}) %copy-start) | copy-done | bytes 1695768
  49.6 0.0 copy-start.1
  49.6 1.0 copy-done.1
  50.6 60.4 %shard_map.47 = f32[192,1104]{1,0:T(8,128)} custom-call(bf16[8,4,24,1104]{3,2,1,0:T(8,128)(2,1)} %bitcast.21, bf16[2,8,3,24,480]{4,3,2,1,0:T(8,128)(2,1)} %bitcast.22), custom_call_target="tpu_custom_call" | custom-call | tf_op jit(solution)/shard_map/pallas_call | solution.py:226
  111.0 1.2 %convert.4 = bf16[192,1104]{1,0:T(8,128)(2,1)S(1)} convert(f32[192,1104]{1,0:T(8,128)} %shard_map.47) | non-fusion elementwise | flops 211968 | bytes 1271808 | tf_op jit(solution)/shard_map/convert.1
  112.2 0.9 convert_element_type.25
  (4 shorter events, 0.1 us)
Async XLA Ops:
  13.7 4.3 %copy-start.3 = (s32[2,20,4,3]{1,2,3,0:T(4,128)S(1)}, s32[2,20,4,3]{1,2,3,0:T(4,128)}, u32[]{:S(2)}) copy-start(s32[2,20,4,3]{1,2,3,0:T(4,128)} %param.7) | copy-start | bytes 5764
  18.0 1.0 copy-start.2
  24.5 2.4 %copy-start.4 = (s32[48,2,4]{0,2,1:T(4,128)S(1)}, s32[48,2,4]{0,2,1:T(4,128)}, u32[]{:S(2)}) copy-start(s32[48,2,4]{0,2,1:T(4,128)} %param.5) | copy-start | bytes 4612
  48.4 1.2 %copy-start = (bf16[4,2,4,24,1104]{4,3,2,1,0:T(8,128)(2,1)}, bf16[4,2,4,24,1104]{4,3,2,1,0:T(8,128)(2,1)S(1)}, u32[]{:S(2)}) copy-start(bf16[4,2,4,24,1104]{4,3,2,1,0:T(8,128)(2,1)S(1)} %get-tuple-element.7) | copy-start | bytes 5087236
  49.6 1.0 copy-start.1

commit v3 on v2

--- a/solution.py
+++ b/solution.py
@@ -11,23 +11,89 @@
 CTW = 32
 
 
-def lay_left(values, columns):
-    rows, panels, slots, square = values.shape
-    edge = math.isqrt(square)
-    blocks = values.reshape(rows, panels, slots, edge, edge).transpose(1, 2, 4, 0, 3)
-    blocks = blocks.reshape(panels, slots, edge, rows * edge)
-    codes = jnp.repeat(columns.transpose(1, 2, 0).astype(jnp.bfloat16), edge, axis=2)
-    return jnp.concatenate([blocks, codes[:, :, None, :]], axis=2)
-
-
-def lay_right(values, columns):
-    panels, rows, tiles, slots, square = values.shape
-    edge = math.isqrt(square)
-    blocks = values.reshape(panels, rows, tiles, slots, edge, edge).transpose(2, 0, 3, 5, 1, 4)
-    blocks = jnp.pad(blocks, ((0, 0),) * 5 + ((0, 1),))
-    blocks = blocks.reshape(tiles, panels, slots, edge, rows * (edge + 1))
-    codes = jnp.repeat(columns.transpose(2, 0, 3, 1).astype(jnp.bfloat16), edge + 1, axis=3)
-    return jnp.concatenate([blocks, codes[:, :, :, None, :]], axis=3)
+LANES = 128
+
+
+def stack_rows(source, at, groups, height, stack_ref, start):
+    block = source.astype(jnp.float32)
+    square = block.shape[1]
+    for tile in range(stack_ref.shape[0]):
+        width = min(LANES, square - tile * LANES)
+        piece = block[:, tile * LANES : tile * LANES + width]
+        if width < LANES:
+            piece = jnp.concatenate([piece, jnp.zeros((groups, LANES - width), jnp.float32)], axis=1)
+        stack_ref[tile, pl.ds(start + at, groups, stride=height), :] = piece
+
+
+def spread(edge, groups, height, rows, pitch, stack_ref, spread_ref):
+    pad = edge + 1
+    tiles = stack_ref.shape[0]
+    span = min(2, tiles)
+    outer = spread_ref.shape[0]
+    source = lax.broadcasted_iota(jnp.int32, (span * LANES, 2 * LANES), 0)
+    lane = lax.broadcasted_iota(jnp.int32, (span * LANES, 2 * LANES), 1)
+    within = lane % LANES % pad
+    offset = jnp.where(within < edge, within + lane // LANES * edge, -1)
+    group = lax.broadcasted_iota(jnp.int32, (height, LANES), 1) // pad
+    for first in range(0, edge, 2):
+        low = min(first * edge // LANES, tiles - span)
+        pick = jnp.where((offset >= 0) & (source + (low * LANES - first * edge) == offset), 1.0, 0.0).astype(jnp.bfloat16)
+        window = jnp.concatenate([stack_ref[low + i].astype(jnp.bfloat16) for i in range(span)], axis=1)
+        moved = jnp.dot(window, pick, preferred_element_type=jnp.float32)
+        for h in range(min(2, edge - first)):
+            for o in range(outer):
+                total = None
+                for g in range(groups):
+                    begin = (o * groups + g) * height
+                    part = moved[begin : begin + height, h * LANES : (h + 1) * LANES]
+                    total = part if total is None else jnp.where(group == g, part, total)
+                spread_ref[o, pl.ds(first + h, rows, stride=pitch), :] = total[:rows, :]
+
+
+def repeat_codes(codes, count, pitch):
+    rows = codes.shape[1]
+    width = rows * pitch
+    source = lax.broadcasted_iota(jnp.int32, (rows, width), 0)
+    lane = lax.broadcasted_iota(jnp.int32, (rows, width), 1)
+    pick = jnp.where((lane >= source * pitch) & (lane < source * pitch + count), 1.0, 0.0).astype(jnp.bfloat16)
+    wide = codes.astype(jnp.float32).astype(jnp.bfloat16)
+    return jnp.dot(wide, pick, preferred_element_type=jnp.float32)
+
+
+def with_codes(turned, code, g, pad):
+    block = turned[g * pad : (g + 1) * pad, :]
+    row = lax.broadcasted_iota(jnp.int32, block.shape, 0)
+    return jnp.where(row == pad - 1, jnp.broadcast_to(code[g : g + 1, :], block.shape), block).astype(jnp.bfloat16)
+
+
+def lay_left(edge, values_ref, codes_ref, stack_ref, spread_ref, put):
+    rows, panels, slots = values_ref.shape[:3]
+    for p in range(panels):
+        for i in range(rows):
+            stack_rows(values_ref[i, p], i, slots, rows, stack_ref, p * slots * rows)
+    spread(edge, slots, rows, rows, edge, stack_ref, spread_ref)
+    for p in range(panels):
+        turned = spread_ref[p].T
+        code = repeat_codes(codes_ref[p], edge, edge)
+        for s in range(slots):
+            put(p, s, with_codes(turned, code, s, edge + 1))
+
+
+def lay_right(edge, values_ref, codes_ref, stack_ref, spread_ref, put):
+    panels, rows, slots, tiles = values_ref.shape[:4]
+    height = -(-rows // 8) * 8
+    for p in range(panels):
+        for s in range(slots):
+            for k in range(rows):
+                stack_rows(values_ref[p, k, s], k, tiles, height, stack_ref, (p * slots + s) * tiles * height)
+    spread_ref[...] = jnp.zeros_like(spread_ref)
+    spread(edge, tiles, height, rows, edge + 1, stack_ref, spread_ref)
+    for p in range(panels):
+        for s in range(slots):
+            turned = spread_ref[p * slots + s].T
+            code = repeat_codes(codes_ref[p, s], edge + 1, edge + 1)
+            for t in range(tiles):
+                put(t, p, s, with_codes(turned, code, t, edge + 1))
 
 
 def expand(values_ref, lead, slots, pad, count, out_ref, base):
@@ -237,7 +303,7 @@
     )(left, right)
 
 
-def gather_kernel(columns, rows, left_ref, right_ref, left_out, right_out, left_send, left_recv, tile_send, tile_recv, row_send, row_recv):
+def gather_kernel(columns, rows, edge, left_values, left_codes, right_values, right_codes, left_out, right_out, left_ref, right_ref, left_stack, left_spread, right_stack, right_spread, left_send, left_recv, tile_send, tile_recv, row_send, row_recv):
     me_col, me_row = lax.axis_index("col"), lax.axis_index("row")
     mesh_id = pl.DeviceIdType.MESH
     barrier = pltpu.get_barrier_semaphore()
@@ -245,6 +311,13 @@
         pl.semaphore_signal(barrier, inc=1, device_id={"col": lax.rem(me_col + d, columns)}, device_id_type=mesh_id)
     for d in range(1, rows):
         pl.semaphore_signal(barrier, inc=1, device_id={"row": lax.rem(me_row + d, rows)}, device_id_type=mesh_id)
+    def put_left(p, slot, block):
+        left_ref[p, slot] = block
+
+    def put_right(t, p, slot, block):
+        right_ref[t, p, slot] = block
+
+    lay_right(edge, right_values, right_codes, right_stack, right_spread, put_right)
     pl.semaphore_wait(barrier, columns + rows - 2)
 
     tile_hops, left_hops, row_hops = [], [], []
@@ -295,6 +368,7 @@
     for hop in tile_hops:
         hop.start()
     to_rows(0, right_ref.at[me_col])
+    lay_left(edge, left_values, left_codes, left_stack, left_spread, put_left)
     for hop in left_hops + passed:
         hop.start()
     left_out[me_col] = left_ref[...]
@@ -314,27 +388,40 @@
         hop.wait_send()
 
 
-def gather(left, right, columns, rows):
+def gather(left_values, left_columns, right_values, right_columns, columns, rows):
     whole = pl.BlockSpec(memory_space=pltpu.VMEM)
     dma = pltpu.SemaphoreType.DMA
+    m_blocks, l_panels, l_slots, square = left_values.shape
+    panels, k_blocks, tiles, slots, _ = right_values.shape
+    edge = math.isqrt(square)
+    pad = edge + 1
+    left = pltpu.VMEM((l_panels, l_slots, pad, m_blocks * edge), jnp.bfloat16)
+    right = pltpu.VMEM((tiles, panels, slots, pad, k_blocks * pad), jnp.bfloat16)
+    deep = -(-square // LANES)
+    height = -(-k_blocks // 8) * 8
     return pl.pallas_call(
-        functools.partial(gather_kernel, columns, rows),
-        in_specs=[whole, whole],
+        functools.partial(gather_kernel, columns, rows, edge),
+        in_specs=[whole] * 4,
         out_specs=[whole, whole],
         out_shape=[
             jax.ShapeDtypeStruct((columns,) + left.shape, left.dtype),
             jax.ShapeDtypeStruct((rows,) + right.shape, right.dtype),
         ],
-        scratch_shapes=[dma((columns,))] * 4 + [dma((rows, columns))] * 2,
+        scratch_shapes=[
+            left,
+            right,
+            pltpu.VMEM((deep, l_panels * l_slots * m_blocks, LANES), jnp.float32),
+            pltpu.VMEM((l_panels, m_blocks * edge, LANES), jnp.float32),
+            pltpu.VMEM((deep, panels * slots * tiles * height, LANES), jnp.float32),
+            pltpu.VMEM((panels * slots, k_blocks * pad, LANES), jnp.float32),
+        ] + [dma((columns,))] * 4 + [dma((rows, columns))] * 2,
         compiler_params=pltpu.CompilerParams(collective_id=1, has_side_effects=True, vmem_limit_bytes=32 << 20),
-    )(left, right)
+    )(left_values, left_columns.transpose(1, 2, 0), right_values.transpose(0, 1, 3, 2, 4), right_columns.transpose(0, 3, 2, 1))
 
 
 def body(columns, rows, depth, left_values, left_columns, right_values, right_columns):
     pad = math.isqrt(left_values.shape[-1]) + 1
-    left, right = gather(
-        lay_left(left_values, left_columns), lay_right(right_values, right_columns), columns, rows
-    )
+    left, right = gather(left_values, left_columns, right_values, right_columns, columns, rows)
     left = left.reshape((-1,) + left.shape[2:])
     right = right.reshape((rows, -1) + right.shape[3:])
     if right_values.shape[1] % 2:

time: 114 us -> 90 us (0.79)
  local copies, waits for them, and re-layouts: 30.2 us -> 6.68 us
    reshape x3 -> x0, local copies, waits for them, and re-layouts: 11.6 us -> none  [the longest x1 4.92 us: lay_right(): values.reshape(panels, rows, tiles, slots, edge, edge)]
    unnamed x12, local copies, waits for them, and re-layouts: 11.2 us -> 5.74 us
    transpose x1 -> x0, local copies, waits for them, and re-layouts: 3.37 us -> none  [lay_left(): values.reshape(rows, panels, slots, edge, edge).transpose(1, 2, 4, 0, 3)]
    pad x1 -> x0, local copies, waits for them, and re-layouts: 2.46 us -> none  [lay_right(): blocks = jnp.pad(blocks, ((0, 0),) * 5 + ((0, 1),))]
where the time goes in v3:
time: 90 us; the launch traced here: 89.7 us
  Pallas kernels  81.8 us (91%)
  local copies, waits for them, and re-layouts  6.68 us (7%)
  other arithmetic  1.22 us (1%)
    pallas_call x1, Pallas kernels, product(): pl.pallas_call(functools.partial(reduce_kernel, pad, n, piece), in_specs=...  60.4 us
    pallas_call x1, Pallas kernels, gather(): pl.pallas_call(functools.partial(gather_kernel, columns, rows, edge), in_...  21.3 us
    unnamed x12, local copies, waits for them, and re-layouts  5.74 us

profile of v3, /device:TPU:8, one launch (start us, length us, event | category | flops | bytes accessed | tf_op | source)
XLA Modules:
  0.0 89.7 jit_solution(9607531992144628495)
XLA Ops:
  0.0 0.0 copy-start.2
  0.0 1.1 %copy-done.2 = bf16[2,20,4,3,529]{4,2,3,1,0:T(4,128)(2,1)S(1)} copy-done((bf16[2,20,4,3,529]{4,2,3,1,0:T(4,128)(2,1)S(1)}, bf16[2,20,4,3,529]{4,2,3,1,0:T(4,128)(2,1)}, u32[]{:S(2)}) %copy-start.2) | copy-done | bytes 507864
  1.1 0.0 copy-start.3
  1.1 1.0 %copy-done.3 = bf16[48,2,4,529]{3,2,1,0:T(4,128)(2,1)S(1)} copy-done((bf16[48,2,4,529]{3,2,1,0:T(4,128)(2,1)S(1)}, bf16[48,2,4,529]{3,2,1,0:T(4,128)(2,1)}, u32[]{:S(2)}) %copy-start.3) | copy-done | bytes 406296
  2.1 0.0 copy-start.4
  2.1 0.7 copy-done.4
  2.8 0.0 copy-start.5
  2.8 0.7 copy-done.5
  3.5 21.3 %shard_map.46 = (bf16[4,2,4,24,1104]{4,3,2,1,0:T(8,128)(2,1)S(1)}, bf16[2,4,2,3,24,480]{5,4,3,2,1,0:T(8,128)(2,1)S(1)}) custom-call(bf16[48,2,4,529]{3,2,1,0:T(4,128)(2,1)S(1)} %copy-done.3, s32[2,4,48]{2,1,0:T(4,128)S(1)} %bitcast.12, bf16[2,20,3,4,529]{4,3,2,1,0:T(4,128)(2,1)S(1)} %bitcast.10, s32[2,3,4,20]{3,2,1,0:T(4,128)S(1)} %bitcast.11), custom_call_target="tpu_custom_call" | custom-call | tf_op jit(solution)/shard_map/pallas_call | solution.py:402
  24.8 0.0 copy-start
  24.9 1.2 %copy-done = bf16[4,2,4,24,1104]{4,3,2,1,0:T(8,128)(2,1)} copy-done((bf16[4,2,4,24,1104]{4,3,2,1,0:T(8,128)(2,1)}, bf16[4,2,4,24,1104]{4,3,2,1,0:T(8,128)(2,1)S(1)}, u32[]{:S(2)}) %copy-start) | copy-done | bytes 1695768
  26.1 0.0 copy-start.1
  26.1 1.0 %copy-done.1 = bf16[2,4,2,3,24,480]{5,4,3,2,1,0:T(8,128)(2,1)} copy-done((bf16[2,4,2,3,24,480]{5,4,3,2,1,0:T(8,128)(2,1)}, bf16[2,4,2,3,24,480]{5,4,3,2,1,0:T(8,128)(2,1)S(1)}, u32[]{:S(2)}) %copy-start.1) | copy-done | bytes 1105944
  27.1 60.4 %shard_map.47 = f32[192,1104]{1,0:T(8,128)} custom-call(bf16[8,4,24,1104]{3,2,1,0:T(8,128)(2,1)} %bitcast.8, bf16[2,8,3,24,480]{4,3,2,1,0:T(8,128)(2,1)} %bitcast.9), custom_call_target="tpu_custom_call" | custom-call | tf_op jit(solution)/shard_map/pallas_call | solution.py:292
  87.5 1.2 %convert.4 = bf16[192,1104]{1,0:T(8,128)(2,1)S(1)} convert(f32[192,1104]{1,0:T(8,128)} %shard_map.47) | non-fusion elementwise | flops 211968 | bytes 1271808 | tf_op jit(solution)/shard_map/convert.1
  88.7 0.9 %convert_element_type.7 = bf16[184,1104]{1,0:T(8,128)(2,1)} reshape(bf16[8,23,1104]{2,1,0:T(8,128)(2,1)S(1)} %bitcast.13) | data formatting | bytes 812544 | tf_op jit(solution)/shard_map/convert_element_type | solution.py:433
Async XLA Ops:
  0.0 1.1 %copy-start.2 = (bf16[2,20,4,3,529]{4,2,3,1,0:T(4,128)(2,1)S(1)}, bf16[2,20,4,3,529]{4,2,3,1,0:T(4,128)(2,1)}, u32[]{:S(2)}) copy-start(bf16[2,20,4,3,529]{4,2,3,1,0:T(4,128)(2,1)} %param.6) | copy-start | bytes 1523524
  1.1 1.0 %copy-start.3 = (bf16[48,2,4,529]{3,2,1,0:T(4,128)(2,1)S(1)}, bf16[48,2,4,529]{3,2,1,0:T(4,128)(2,1)}, u32[]{:S(2)}) copy-start(bf16[48,2,4,529]{3,2,1,0:T(4,128)(2,1)} %left_values.1) | copy-start | bytes 1218820
  2.1 0.7 copy-start.4
  2.8 0.7 copy-start.5
  24.8 1.2 %copy-start = (bf16[4,2,4,24,1104]{4,3,2,1,0:T(8,128)(2,1)}, bf16[4,2,4,24,1104]{4,3,2,1,0:T(8,128)(2,1)S(1)}, u32[]{:S(2)}) copy-start(bf16[4,2,4,24,1104]{4,3,2,1,0:T(8,128)(2,1)S(1)} %get-tuple-element.7) | copy-start | bytes 5087236
  26.1 1.0 %copy-start.1 = (bf16[2,4,2,3,24,480]{5,4,3,2,1,0:T(8,128)(2,1)}, bf16[2,4,2,3,24,480]{5,4,3,2,1,0:T(8,128)(2,1)S(1)}, u32[]{:S(2)}) copy-start(bf16[2,4,2,3,24,480]{5,4,3,2,1,0:T(8,128)(2,1)S(1)} %get-tuple-element.8) | copy-start | bytes 3317764

commit v4 on v3

v4 whole, which is shorter than its diff:
```python
import functools
import math

import jax
import jax.numpy as jnp
from jax import lax
from jax.experimental import pallas as pl
from jax.experimental.pallas import tpu as pltpu
from jax.sharding import PartitionSpec as P

CTW = 32


LANES = 128


def stack_rows(source, at, groups, height, stack_ref, start):
    block = source.astype(jnp.float32)
    square = block.shape[1]
    for tile in range(stack_ref.shape[0]):
        width = min(LANES, square - tile * LANES)
        piece = block[:, tile * LANES : tile * LANES + width]
        if width < LANES:
            piece = jnp.concatenate([piece, jnp.zeros((groups, LANES - width), jnp.float32)], axis=1)
        stack_ref[tile, pl.ds(start + at, groups, stride=height), :] = piece


def spread(edge, groups, height, rows, pitch, stack_ref, spread_ref):
    pad = edge + 1
    tiles = stack_ref.shape[0]
    span = min(2, tiles)
    outer = spread_ref.shape[0]
    source = lax.broadcasted_iota(jnp.int32, (span * LANES, 2 * LANES), 0)
    lane = lax.broadcasted_iota(jnp.int32, (span * LANES, 2 * LANES), 1)
    within = lane % LANES % pad
    offset = jnp.where(within < edge, within + lane // LANES * edge, -1)
    group = lax.broadcasted_iota(jnp.int32, (height, LANES), 1) // pad
    for first in range(0, edge, 2):
        low = min(first * edge // LANES, tiles - span)
        pick = jnp.where((offset >= 0) & (source + (low * LANES - first * edge) == offset), 1.0, 0.0).astype(jnp.bfloat16)
        window = jnp.concatenate([stack_ref[low + i].astype(jnp.bfloat16) for i in range(span)], axis=1)
        moved = jnp.dot(window, pick, preferred_element_type=jnp.float32)
        for h in range(min(2, edge - first)):
            for o in range(outer):
                total = None
                for g in range(groups):
                    begin = (o * groups + g) * height
                    part = moved[begin : begin + height, h * LANES : (h + 1) * LANES]
                    total = part if total is None else jnp.where(group == g, part, total)
                spread_ref[o, pl.ds(first + h, rows, stride=pitch), :] = total[:rows, :]


def repeat_codes(codes, count, pitch):
    rows = codes.shape[1]
    width = rows * pitch
    source = lax.broadcasted_iota(jnp.int32, (rows, width), 0)
    lane = lax.broadcasted_iota(jnp.int32, (rows, width), 1)
    pick = jnp.where((lane >= source * pitch) & (lane < source * pitch + count), 1.0, 0.0).astype(jnp.bfloat16)
    wide = codes.astype(jnp.float32).astype(jnp.bfloat16)
    return jnp.dot(wide, pick, preferred_element_type=jnp.float32)


def with_codes(turned, code, g, pad):
    block = turned[g * pad : (g + 1) * pad, :]
    row = lax.broadcasted_iota(jnp.int32, block.shape, 0)
    return jnp.where(row == pad - 1, jnp.broadcast_to(code[g : g + 1, :], block.shape), block).astype(jnp.bfloat16)


def lay_left(edge, values_ref, codes_ref, stack_ref, spread_ref, put):
    rows, panels, slots = values_ref.shape[:3]
    for p in range(panels):
        for i in range(rows):
            stack_rows(values_ref[i, p], i, slots, rows, stack_ref, p * slots * rows)
    spread(edge, slots, rows, rows, edge, stack_ref, spread_ref)
    for p in range(panels):
        turned = spread_ref[p].T
        code = repeat_codes(codes_ref[p], edge, edge)
        for s in range(slots):
            put(p, s, with_codes(turned, code, s, edge + 1))


def lay_right(edge, values_ref, codes_ref, stack_ref, spread_ref, put):
    panels, rows, slots, tiles = values_ref.shape[:4]
    height = -(-rows // 8) * 8
    for p in range(panels):
        for s in range(slots):
            for k in range(rows):
                stack_rows(values_ref[p, k, s], k, tiles, height, stack_ref, (p * slots + s) * tiles * height)
    spread_ref[...] = jnp.zeros_like(spread_ref)
    spread(edge, tiles, height, rows, edge + 1, stack_ref, spread_ref)
    for p in range(panels):
        for s in range(slots):
            turned = spread_ref[p * slots + s].T
            code = repeat_codes(codes_ref[p, s], edge + 1, edge + 1)
            for t in range(tiles):
                put(t, p, s, with_codes(turned, code, t, edge + 1))


def expand(values_ref, lead, slots, pad, count, out_ref, base):
    width = out_ref.shape[-1]
    lower = lax.broadcasted_iota(jnp.int32, (2 * pad, width), 0) >= pad
    shift = jnp.where(lower, 1.0, 0.0)
    doubled, codes = [], []
    for s in range(slots):
        one = values_ref[lead + (s,)].astype(jnp.float32)
        code = jnp.broadcast_to(one[pad - 1 : pad, :], (2 * pad, width)) - shift
        doubled.append(jnp.concatenate([one, one], axis=0).astype(jnp.bfloat16))
        codes.append(code.astype(jnp.bfloat16))
    for pair in range(-(-count // 2)):
        high = min(2 * pad, (count - 2 * pair) * pad)
        want = jnp.bfloat16(base + 2 * pair)
        filled = jnp.zeros((2 * pad, width), jnp.bfloat16)
        for s in range(slots):
            filled = jnp.where(codes[s] == want, doubled[s], filled)
        out_ref[2 * pad * pair : 2 * pad * pair + high, :] = filled[:high, :]


FULL = 32700.0


def encode(x, pad):
    row = lax.broadcasted_iota(jnp.int32, x.shape, 0)
    x = jnp.where(row % pad == pad - 1, 0.0, x)
    most = jnp.maximum(jnp.max(jnp.abs(x), axis=0, keepdims=True), 1e-30)
    power = jnp.floor(jnp.log2(most)) + 1.0
    coded = jnp.round(x * (jnp.exp2(-power) * FULL))
    return jnp.where(row == pad - 1, power, coded).astype(jnp.int32).astype(jnp.int16)


def decode(coded, pad):
    x = coded.astype(jnp.int32).astype(jnp.float32)
    return x * (jnp.exp2(x[pad - 1 : pad, :]) * (1.0 / FULL))


def kernel(columns, rows, n, edge, piece, left_hbm, left_code_hbm, right_hbm, right_code_hbm, out_ref, left_values, left_codes, right_values, right_codes, left_in, right_own, right_in, left_stack, left_spread, right_stack, right_spread, left_dense, right_dense, sums, r_out, r_in, l_out, l_in, load_sem, left_send, left_recv, tile_send, tile_recv, row_send, row_recv, r_send, r_recv, l_send, l_recv):
    me_col, me_row, me = lax.axis_index("col"), lax.axis_index("row"), lax.axis_index("depth")
    mesh_id = pl.DeviceIdType.MESH
    pad = edge + 1
    loads = [
        pltpu.make_async_copy(source, target, load_sem.at[i])
        for i, (source, target) in enumerate(
            [(right_hbm, right_values), (right_code_hbm, right_codes), (left_hbm, left_values), (left_code_hbm, left_codes)]
        )
    ]
    for load in loads:
        load.start()
    barrier = pltpu.get_barrier_semaphore()
    for d in range(1, columns):
        pl.semaphore_signal(barrier, inc=1, device_id={"col": lax.rem(me_col + d, columns)}, device_id_type=mesh_id)
    for d in range(1, rows):
        pl.semaphore_signal(barrier, inc=1, device_id={"row": lax.rem(me_row + d, rows)}, device_id_type=mesh_id)

    @pl.when(me > 0)
    def _():
        pl.semaphore_signal(barrier, inc=1, device_id={"depth": me - 1}, device_id_type=mesh_id)

    @pl.when(me < n - 1)
    def _():
        pl.semaphore_signal(barrier, inc=1, device_id={"depth": me + 1}, device_id_type=mesh_id)

    def put_left(p, slot, block):
        left_in[me_col, p, slot] = block

    def put_right(t, p, slot, block):
        right_own[t, p, slot] = block

    loads[0].wait()
    loads[1].wait()
    lay_right(edge, right_values, right_codes, right_stack, right_spread, put_right)
    pl.semaphore_wait(barrier, columns + rows - 2 + jnp.where(me > 0, 1, 0) + jnp.where(me < n - 1, 1, 0))

    tile_hops = []
    for d in range(1, columns):
        other = lax.rem(me_col + d, columns)
        tile_hops.append(
            pltpu.make_async_remote_copy(
                src_ref=right_own.at[other],
                dst_ref=right_in.at[me_row, me_col],
                send_sem=tile_send.at[d],
                recv_sem=tile_recv.at[d],
                device_id={"col": other},
                device_id_type=mesh_id,
            )
        )

    paired = columns % 2 == 0
    partner = me_col + 1 - 2 * lax.rem(me_col, 2)

    def left_hop(i, slot, other):
        return pltpu.make_async_remote_copy(
            src_ref=left_in.at[slot],
            dst_ref=left_in.at[slot],
            send_sem=left_send.at[i],
            recv_sem=left_recv.at[i],
            device_id={"col": other},
            device_id_type=mesh_id,
        )

    strides = range(2, columns, 2) if paired else range(1, columns)
    left_hops = [left_hop(d, me_col, lax.rem(me_col + d, columns)) for d in strides]
    passed = [left_hop(1, me_col, partner)] if paired else []
    row_hops = {}

    def back(d):
        return lax.rem(me_col + columns - d, columns)

    def to_rows(d, source):
        for e in range(1, rows):
            hop = pltpu.make_async_remote_copy(
                src_ref=source,
                dst_ref=right_in.at[me_row, back(d)],
                send_sem=row_send.at[e, d],
                recv_sem=row_recv.at[e, d],
                device_id={"row": lax.rem(me_row + e, rows)},
                device_id_type=mesh_id,
            )
            hop.start()
            row_hops[d, e] = hop

    for hop in tile_hops:
        hop.start()
    to_rows(0, right_own.at[me_col])
    loads[2].wait()
    loads[3].wait()
    lay_left(edge, left_values, left_codes, left_stack, left_spread, put_left)
    for hop in left_hops + passed:
        hop.start()
    right_in[me_row, me_col] = right_own[me_col]

    panels, slots_l = left_in.shape[1:3]
    slots_r = right_in.shape[3]
    here = left_dense.shape[2] // pad
    wide = sums.shape[1]
    per = wide // pad
    pieces = wide // piece
    total = (n - 1) * pieces

    def fill_left(slot):
        def one(p, carry):
            for r in range(rows):
                expand(left_in, (slot, p), slots_l, pad, here, left_dense.at[slot * panels + p, r], r * here)
            return carry

        lax.fori_loop(0, panels, one, 0)

    def add_products(d, slot):
        def fill(p, carry):
            for r in range(rows):
                expand(right_in, (r, slot, p), slots_r, pad, per, right_dense.at[slot * panels + p, r], d * per)
            return carry

        lax.fori_loop(0, panels, fill, 0)

        def add(p, carry):
            total = sums[d]
            for r in range(rows):
                total += jnp.dot(right_dense[slot * panels + p, r], left_dense[slot * panels + p, r], preferred_element_type=jnp.float32)
            sums[d] = total
            return carry

        lax.fori_loop(0, panels, add, 0)

    after, before = n - 1 - me, me
    lead = jnp.where(after >= before, after - before, before - after)
    near = jnp.where(after >= before, before, after)

    def order(step):
        s = step - lead
        distance = near - s // 2
        paired = jnp.where(s % 2 == 0, me + distance, me - distance)
        alone = jnp.where(after >= before, n - 1 - step, step)
        return jnp.where(step < lead, alone, paired)

    def span(i):
        return pl.ds(pl.multiple_of(i * piece, piece), piece)

    def right_hop(t, i):
        return pltpu.make_async_remote_copy(
            src_ref=r_out.at[t, span(i)],
            dst_ref=r_in.at[t, span(i)],
            send_sem=r_send.at[t, i],
            recv_sem=r_recv.at[t, i],
            device_id={"depth": me + 1},
            device_id_type=mesh_id,
        )

    def depth_left_hop(t, i):
        return pltpu.make_async_remote_copy(
            src_ref=l_out.at[t, span(i)],
            dst_ref=l_in.at[t, span(i)],
            send_sem=l_send.at[t, i],
            recv_sem=l_recv.at[t, i],
            device_id={"depth": me - 1},
            device_id_type=mesh_id,
        )

    def send_own(d):
        @pl.when((me == 0) & (d > 0))
        def _():
            def send(i, inner):
                r_out[n - 1 - d, span(i), :] = encode(sums[d, span(i), :], pad)
                right_hop(n - 1 - d, i).start()
                return inner

            lax.fori_loop(0, pieces, send, 0)

        @pl.when((me == n - 1) & (d < n - 1))
        def _():
            def send(i, inner):
                l_out[d, span(i), :] = encode(sums[d, span(i), :], pad)
                depth_left_hop(d, i).start()
                return inner

            lax.fori_loop(0, pieces, send, 0)

    first = order(0)
    sums[first] = jnp.zeros(sums.shape[1:], jnp.float32)
    fill_left(me_col)
    for d, hop in enumerate(tile_hops, 1):
        hop.wait_recv()
        to_rows(d, right_in.at[me_row, back(d)])
    if paired:
        passed[0].wait_recv()
        fill_left(partner)
    for d, hop in zip(strides, left_hops):
        hop.wait_recv()
        if paired:
            passed.append(left_hop(d + 1, back(d), partner))
            passed[-1].start()
        fill_left(back(d))
    sources = [me_col] + ([partner] if paired else []) + [back(d) for d in strides]
    late = []
    if paired:
        for hop, d in zip(passed[1:], strides):
            late.append((hop, lax.rem(partner + columns - d, columns)))
    for d in range(columns):
        for e in range(1, rows):
            row_hops[d, e].wait_recv()
    for slot in sources:
        add_products(first, slot)
    for hop, slot in late:
        hop.wait_recv()
        fill_left(slot)
        add_products(first, slot)
    send_own(first)

    def chunk_step(step, carry):
        d = order(step)
        sums[d] = jnp.zeros(sums.shape[1:], jnp.float32)

        def each(slot, inner):
            add_products(d, slot)
            return inner

        lax.fori_loop(0, columns, each, 0)
        send_own(d)
        return carry

    lax.fori_loop(1, n, chunk_step, 0)

    lag = 2

    def pass_on(step, carry):
        q = step - lag * me
        t, i = q // pieces, q % pieces
        d = n - 1 - t

        @pl.when((q >= 0) & (q < total) & (me > 0) & (me <= d))
        def _():
            right_hop(t, i).wait_recv()
            sums[d, span(i), :] += decode(r_in[t, span(i), :], pad)

            @pl.when(me < d)
            def _():
                r_out[t, span(i), :] = encode(sums[d, span(i), :], pad)
                right_hop(t, i).start()

        k = step - lag * (n - 1 - me)
        u, j = k // pieces, k % pieces

        @pl.when((k >= 0) & (k < total) & (me < n - 1) & (me >= u))
        def _():
            depth_left_hop(u, j).wait_recv()
            sums[u, span(j), :] += decode(l_in[u, span(j), :], pad)

            @pl.when(me > u)
            def _():
                l_out[u, span(j), :] = encode(sums[u, span(j), :], pad)
                depth_left_hop(u, j).start()

        return carry

    lax.fori_loop(0, total + lag * (n - 1), pass_on, 0)
    for j in range(per):
        out_ref[edge * j : edge * (j + 1), :] = sums[me, pad * j : pad * j + edge, :].astype(out_ref.dtype)

    def drain(step, carry):
        t, i = step // pieces, step % pieces

        @pl.when(me < n - 1 - t)
        def _():
            right_hop(t, i).wait_send()

        @pl.when(me > t)
        def _():
            depth_left_hop(t, i).wait_send()

        return carry

    lax.fori_loop(0, total, drain, 0)
    for hop in tile_hops + left_hops + passed + list(row_hops.values()):
        hop.wait_send()


def body(columns, rows, n, left_values, left_columns, right_values, right_columns):
    m_blocks, panels, l_slots, square = left_values.shape
    _, k_blocks, tiles, slots, _ = right_values.shape
    edge = math.isqrt(square)
    pad = edge + 1
    m = m_blocks * edge
    k = k_blocks * pad
    deep = -(-square // LANES)
    height = -(-k_blocks // 8) * 8
    wide = CTW // n * pad
    piece = 2 * pad
    pieces = wide // piece
    operands = (left_values, left_columns.transpose(1, 2, 0), right_values.transpose(0, 1, 3, 2, 4), right_columns.transpose(0, 3, 2, 1))
    travel = pltpu.VMEM((n - 1, wide, m), jnp.int16)
    dma = pltpu.SemaphoreType.DMA
    result = pl.pallas_call(
        functools.partial(kernel, columns, rows, n, edge, piece),
        in_specs=[pl.BlockSpec(memory_space=pl.ANY)] * 4,
        out_specs=pl.BlockSpec(memory_space=pltpu.VMEM),
        out_shape=jax.ShapeDtypeStruct((CTW // n * edge, m), jnp.bfloat16),
        scratch_shapes=[pltpu.VMEM(x.shape, x.dtype) for x in operands]
        + [
            pltpu.VMEM((columns, panels, l_slots, pad, m), jnp.bfloat16),
            pltpu.VMEM((tiles, panels, slots, pad, k), jnp.bfloat16),
            pltpu.VMEM((rows, columns, panels, slots, pad, k), jnp.bfloat16),
            pltpu.VMEM((deep, panels * l_slots * m_blocks, LANES), jnp.float32),
            pltpu.VMEM((panels, m, LANES), jnp.float32),
            pltpu.VMEM((deep, panels * slots * tiles * height, LANES), jnp.float32),
            pltpu.VMEM((panels * slots, k, LANES), jnp.float32),
            pltpu.VMEM((columns * panels, rows, k, m), jnp.bfloat16),
            pltpu.VMEM((columns * panels, rows, wide, k), jnp.bfloat16),
            pltpu.VMEM((n, wide, m), jnp.float32),
        ]
        + [travel] * 4
        + [dma((4,))]
        + [dma((columns,))] * 4
        + [dma((rows, columns))] * 2
        + [dma((n - 1, pieces))] * 4,
        compiler_params=pltpu.CompilerParams(collective_id=0, has_side_effects=True, vmem_limit_bytes=56 << 20),
    )(*operands)
    return result.T


def solution(mesh):
    placed = (
        P("row", ("col", "depth"), None, None),
        P("row", ("col", "depth"), None),
        P(("col", "depth"), "row", None, None, None),
        P(("col", "depth"), "row", None, None),
    )
    return jax.shard_map(
        functools.partial(body, mesh.shape["col"], mesh.shape["row"], mesh.shape["depth"]), mesh=mesh, in_specs=placed, out_specs=P("row", ("col", "depth")), check_vma=False
    )
```

time: 90 us -> 75.5 us (0.84)
  Pallas kernels: 81.8 us -> 73.5 us
  local copies, waits for them, and re-layouts: 6.68 us -> 1.79 us
  other arithmetic: 1.22 us -> 0 us
    pallas_call x2 -> x1, Pallas kernels: 81.8 us -> 73.5 us  [body(): pl.pallas_call(functools.partial(kernel, columns, rows, n, edge, piece),...]
    unnamed x12 -> x1, local copies, waits for them, and re-layouts: 5.74 us -> 1.79 us
    another operation x1 -> x0, other arithmetic: 1.22 us -> none
    convert_element_type x1 -> x0, local copies, waits for them, and re-layouts: 0.94 us -> none  [body(): return result.T.astype(jnp.bfloat16)]
where the time goes in v4:
time: 75.5 us; the launch traced here: 75.3 us
  Pallas kernels  73.5 us (97%)
  local copies, waits for them, and re-layouts  1.79 us (2%)
    pallas_call x1, Pallas kernels, body(): pl.pallas_call(functools.partial(kernel, columns, rows, n, edge, piece),...  73.5 us
    unnamed x1, local copies, waits for them, and re-layouts  1.79 us

profile of v4, /device:TPU:8, one launch (start us, length us, event | category | flops | bytes accessed | tf_op | source)
XLA Modules:
  0.0 75.3 jit_solution(3373388727518810895)
XLA Ops:
  0.0 73.5 %shard_map.46 = bf16[184,1104]{1,0:T(8,128)(2,1)} custom-call(bf16[48,2,4,529]{3,2,1,0:T(4,128)(2,1)} %left_hbm.1, s32[2,4,48]{2,1,0:T(4,128)} %bitcast.7, bf16[2,20,3,4,529]{4,3,2,1,0:T(4,128)(2,1)} %bitcast.5, s32[2,3,4,20]{3,2,1,0:T(4,128)} %bitcast.6), custom_call_target="tpu_custom_call" | custom-call | tf_op jit(solution)/shard_map/pallas_call | solution.py:430
  73.5 1.8 %copy.6 = bf16[1104,184]{0,1:T(8,128)(2,1)} copy(bf16[1104,184]{0,1:T(8,128)(2,1)} %bitcast.4) | data formatting | bytes 812544

commit v5 on v4

--- a/solution.py
+++ b/solution.py
@@ -169,65 +169,77 @@
     lay_right(edge, right_values, right_codes, right_stack, right_spread, put_right)
     pl.semaphore_wait(barrier, columns + rows - 2 + jnp.where(me > 0, 1, 0) + jnp.where(me < n - 1, 1, 0))
 
-    tile_hops = []
-    for d in range(1, columns):
-        other = lax.rem(me_col + d, columns)
-        tile_hops.append(
-            pltpu.make_async_remote_copy(
-                src_ref=right_own.at[other],
-                dst_ref=right_in.at[me_row, me_col],
-                send_sem=tile_send.at[d],
-                recv_sem=tile_recv.at[d],
-                device_id={"col": other},
-                device_id_type=mesh_id,
-            )
-        )
-
     paired = columns % 2 == 0
     partner = me_col + 1 - 2 * lax.rem(me_col, 2)
-
-    def left_hop(i, slot, other):
+    strides = range(2, columns, 2) if paired else range(1, columns)
+    panels, slots_l = left_in.shape[1:3]
+
+    def back(d):
+        return lax.rem(me_col + columns - d, columns)
+
+    def tile_hop(other, origin):
         return pltpu.make_async_remote_copy(
-            src_ref=left_in.at[slot],
-            dst_ref=left_in.at[slot],
-            send_sem=left_send.at[i],
-            recv_sem=left_recv.at[i],
+            src_ref=right_own.at[other],
+            dst_ref=right_in.at[me_row, origin],
+            send_sem=tile_send.at[other],
+            recv_sem=tile_recv.at[origin],
             device_id={"col": other},
             device_id_type=mesh_id,
         )
 
-    strides = range(2, columns, 2) if paired else range(1, columns)
-    left_hops = [left_hop(d, me_col, lax.rem(me_col + d, columns)) for d in strides]
-    passed = [left_hop(1, me_col, partner)] if paired else []
-    row_hops = {}
-
-    def back(d):
-        return lax.rem(me_col + columns - d, columns)
-
-    def to_rows(d, source):
+    def left_hop(slot, p, other):
+        return pltpu.make_async_remote_copy(
+            src_ref=left_in.at[slot, p],
+            dst_ref=left_in.at[slot, p],
+            send_sem=left_send.at[lax.rem(other + columns - slot, columns), p],
+            recv_sem=left_recv.at[slot, p],
+            device_id={"col": other},
+            device_id_type=mesh_id,
+        )
+
+    def row_hop(e, slot, source):
+        return pltpu.make_async_remote_copy(
+            src_ref=source,
+            dst_ref=right_in.at[me_row, slot],
+            send_sem=row_send.at[e, slot],
+            recv_sem=row_recv.at[e, slot],
+            device_id={"row": lax.rem(me_row + e, rows)},
+            device_id_type=mesh_id,
+        )
+
+    sent = []
+
+    def go(hop):
+        hop.start()
+        sent.append(hop)
+
+    def to_rows(slot, source):
         for e in range(1, rows):
-            hop = pltpu.make_async_remote_copy(
-                src_ref=source,
-                dst_ref=right_in.at[me_row, back(d)],
-                send_sem=row_send.at[e, d],
-                recv_sem=row_recv.at[e, d],
-                device_id={"row": lax.rem(me_row + e, rows)},
-                device_id_type=mesh_id,
-            )
-            hop.start()
-            row_hops[d, e] = hop
-
-    for hop in tile_hops:
-        hop.start()
-    to_rows(0, right_own.at[me_col])
+            go(row_hop(e, slot, source))
+
+    def pass_tile(slot):
+        tile_hop(slot, slot).wait_recv()
+        to_rows(slot, right_in.at[me_row, slot])
+
+    def wait_rows(slot):
+        for e in range(1, rows):
+            row_hop(e, slot, right_in.at[me_row, slot]).wait_recv()
+
+    near = [back(d) for d in strides]
+    late = [lax.rem(partner + columns - d, columns) for d in strides] if paired else []
+    for slot in near + late + ([partner] if paired else []):
+        go(tile_hop(slot, me_col))
+    to_rows(me_col, right_own.at[me_col])
     loads[2].wait()
     loads[3].wait()
     lay_left(edge, left_values, left_codes, left_stack, left_spread, put_left)
-    for hop in left_hops + passed:
-        hop.start()
+    for p in range(panels):
+        for d in strides:
+            go(left_hop(me_col, p, lax.rem(me_col + d, columns)))
+        if paired:
+            go(left_hop(me_col, p, partner))
     right_in[me_row, me_col] = right_own[me_col]
 
-    panels, slots_l = left_in.shape[1:3]
     slots_r = right_in.shape[3]
     here = left_dense.shape[2] // pad
     wide = sums.shape[1]
@@ -235,38 +247,32 @@
     pieces = wide // piece
     total = (n - 1) * pieces
 
-    def fill_left(slot):
+    def fill_left(slot, p):
+        for r in range(rows):
+            expand(left_in, (slot, p), slots_l, pad, here, left_dense.at[slot * panels + p, r], r * here)
+
+    def add_products(d, q):
+        for r in range(rows):
+            expand(right_in, (r, q // panels, q % panels), slots_r, pad, per, right_dense.at[r], d * per)
+        total = sums[d]
+        for r in range(rows):
+            total += jnp.dot(right_dense[r], left_dense[q, r], preferred_element_type=jnp.float32)
+        sums[d] = total
+
+    def each_panel(step):
         def one(p, carry):
-            for r in range(rows):
-                expand(left_in, (slot, p), slots_l, pad, here, left_dense.at[slot * panels + p, r], r * here)
+            step(p)
             return carry
 
         lax.fori_loop(0, panels, one, 0)
-
-    def add_products(d, slot):
-        def fill(p, carry):
-            for r in range(rows):
-                expand(right_in, (r, slot, p), slots_r, pad, per, right_dense.at[slot * panels + p, r], d * per)
-            return carry
-
-        lax.fori_loop(0, panels, fill, 0)
-
-        def add(p, carry):
-            total = sums[d]
-            for r in range(rows):
-                total += jnp.dot(right_dense[slot * panels + p, r], left_dense[slot * panels + p, r], preferred_element_type=jnp.float32)
-            sums[d] = total
-            return carry
-
-        lax.fori_loop(0, panels, add, 0)
 
     after, before = n - 1 - me, me
     lead = jnp.where(after >= before, after - before, before - after)
-    near = jnp.where(after >= before, before, after)
+    close = jnp.where(after >= before, before, after)
 
     def order(step):
         s = step - lead
-        distance = near - s // 2
+        distance = close - s // 2
         paired = jnp.where(s % 2 == 0, me + distance, me - distance)
         alone = jnp.where(after >= before, n - 1 - step, step)
         return jnp.where(step < lead, alone, paired)
@@ -315,48 +321,36 @@
 
     first = order(0)
     sums[first] = jnp.zeros(sums.shape[1:], jnp.float32)
-    fill_left(me_col)
-    for d, hop in enumerate(tile_hops, 1):
-        hop.wait_recv()
-        to_rows(d, right_in.at[me_row, back(d)])
     if paired:
-        passed[0].wait_recv()
-        fill_left(partner)
-    for d, hop in zip(strides, left_hops):
-        hop.wait_recv()
-        if paired:
-            passed.append(left_hop(d + 1, back(d), partner))
-            passed[-1].start()
-        fill_left(back(d))
-    sources = [me_col] + ([partner] if paired else []) + [back(d) for d in strides]
-    late = []
+        pass_tile(partner)
+    each_panel(lambda p: fill_left(me_col, p))
+    wait_rows(me_col)
+    each_panel(lambda p: add_products(first, me_col * panels + p))
+    for slot in near + late:
+        pass_tile(slot)
     if paired:
-        for hop, d in zip(passed[1:], strides):
-            late.append((hop, lax.rem(partner + columns - d, columns)))
-    for d in range(columns):
-        for e in range(1, rows):
-            row_hops[d, e].wait_recv()
-    for slot in sources:
-        add_products(first, slot)
-    for hop, slot in late:
-        hop.wait_recv()
-        fill_left(slot)
-        add_products(first, slot)
+        for p in range(panels):
+            left_hop(partner, p, partner).wait_recv()
+        each_panel(lambda p: fill_left(partner, p))
+        wait_rows(partner)
+        each_panel(lambda p: add_products(first, partner * panels + p))
+    for p in range(panels):
+        for slot in near:
+            left_hop(slot, p, partner).wait_recv()
+            if paired:
+                go(left_hop(slot, p, partner))
+        for slot in near:
+            fill_left(slot, p)
+            if p == 0:
+                wait_rows(slot)
+            add_products(first, slot * panels + p)
+        for slot in late:
+            left_hop(slot, p, partner).wait_recv()
+            fill_left(slot, p)
+            if p == 0:
+                wait_rows(slot)
+            add_products(first, slot * panels + p)
     send_own(first)
-
-    def chunk_step(step, carry):
-        d = order(step)
-        sums[d] = jnp.zeros(sums.shape[1:], jnp.float32)
-
-        def each(slot, inner):
-            add_products(d, slot)
-            return inner
-
-        lax.fori_loop(0, columns, each, 0)
-        send_own(d)
-        return carry
-
-    lax.fori_loop(1, n, chunk_step, 0)
 
     lag = 2
 
@@ -390,7 +384,27 @@
 
         return carry
 
-    lax.fori_loop(0, total + lag * (n - 1), pass_on, 0)
+    lax.fori_loop(0, 1, pass_on, 0)
+
+    def chunk_step(step, carry):
+        d = order(step)
+        sums[d] = jnp.zeros(sums.shape[1:], jnp.float32)
+
+        def each(q, inner):
+            add_products(d, q)
+            return inner
+
+        lax.fori_loop(0, columns * panels, each, 0)
+        send_own(d)
+
+        @pl.when(step < n - 1)
+        def _():
+            lax.fori_loop(2 * step - 1, 2 * step + 1, pass_on, 0)
+
+        return carry
+
+    lax.fori_loop(1, n, chunk_step, 0)
+    lax.fori_loop(2 * n - 3, total + lag * (n - 1), pass_on, 0)
     for j in range(per):
         out_ref[edge * j : edge * (j + 1), :] = sums[me, pad * j : pad * j + edge, :].astype(out_ref.dtype)
 
@@ -408,7 +422,7 @@
         return carry
 
     lax.fori_loop(0, total, drain, 0)
-    for hop in tile_hops + left_hops + passed + list(row_hops.values()):
+    for hop in sent:
         hop.wait_send()
 
 
@@ -442,12 +456,13 @@
             pltpu.VMEM((deep, panels * slots * tiles * height, LANES), jnp.float32),
             pltpu.VMEM((panels * slots, k, LANES), jnp.float32),
             pltpu.VMEM((columns * panels, rows, k, m), jnp.bfloat16),
-            pltpu.VMEM((columns * panels, rows, wide, k), jnp.bfloat16),
+            pltpu.VMEM((rows, wide, k), jnp.bfloat16),
             pltpu.VMEM((n, wide, m), jnp.float32),
         ]
         + [travel] * 4
         + [dma((4,))]
-        + [dma((columns,))] * 4
+        + [dma((columns, panels))] * 2
+        + [dma((columns,))] * 2
         + [dma((rows, columns))] * 2
         + [dma((n - 1, pieces))] * 4,
         compiler_params=pltpu.CompilerParams(collective_id=0, has_side_effects=True, vmem_limit_bytes=56 << 20),

time: 75.5 us -> 59.9 us (0.79)
  Pallas kernels: 73.5 us -> 57.9 us
    pallas_call x1, Pallas kernels: 73.5 us -> 57.9 us  [body(): pl.pallas_call(functools.partial(kernel, columns, rows, n, edge, piece),...]
where the time goes in v5:
time: 59.9 us; the launch traced here: 59.7 us
  Pallas kernels  57.9 us (97%)
  local copies, waits for them, and re-layouts  1.79 us (3%)
    pallas_call x1, Pallas kernels, body(): pl.pallas_call(functools.partial(kernel, columns, rows, n, edge, piece),...  57.9 us
    unnamed x1, local copies, waits for them, and re-layouts  1.79 us

profile of v5, /device:TPU:8, one launch (start us, length us, event | category | flops | bytes accessed | tf_op | source)
XLA Modules:
  0.0 59.7 jit_solution(14406387575451256450)
XLA Ops:
  0.0 57.9 %shard_map.46 = bf16[184,1104]{1,0:T(8,128)(2,1)} custom-call(bf16[48,2,4,529]{3,2,1,0:T(4,128)(2,1)} %left_hbm.1, s32[2,4,48]{2,1,0:T(4,128)} %bitcast.7, bf16[2,20,3,4,529]{4,3,2,1,0:T(4,128)(2,1)} %bitcast.5, s32[2,3,4,20]{3,2,1,0:T(4,128)} %bitcast.6), custom_call_target="tpu_custom_call" | custom-call | tf_op jit(solution)/shard_map/pallas_call | solution.py:444
  57.9 1.8 %copy.6 = bf16[1104,184]{0,1:T(8,128)(2,1)} copy(bf16[1104,184]{0,1:T(8,128)(2,1)} %bitcast.4) | data formatting | bytes 812544

commit v6 on v5

--- a/solution.py
+++ b/solution.py
@@ -79,21 +79,22 @@
             put(p, s, with_codes(turned, code, s, edge + 1))
 
 
-def lay_right(edge, values_ref, codes_ref, stack_ref, spread_ref, put):
+def lay_right(edge, values_ref, codes_ref, stack_ref, spread_ref, put, ready):
     panels, rows, slots, tiles = values_ref.shape[:4]
     height = -(-rows // 8) * 8
+    deep = slots * tiles * height
+    spread_ref[...] = jnp.zeros_like(spread_ref)
     for p in range(panels):
         for s in range(slots):
             for k in range(rows):
                 stack_rows(values_ref[p, k, s], k, tiles, height, stack_ref, (p * slots + s) * tiles * height)
-    spread_ref[...] = jnp.zeros_like(spread_ref)
-    spread(edge, tiles, height, rows, edge + 1, stack_ref, spread_ref)
-    for p in range(panels):
+        spread(edge, tiles, height, rows, edge + 1, stack_ref.at[:, p * deep : (p + 1) * deep], spread_ref.at[p * slots : (p + 1) * slots])
         for s in range(slots):
             turned = spread_ref[p * slots + s].T
             code = repeat_codes(codes_ref[p, s], edge + 1, edge + 1)
             for t in range(tiles):
                 put(t, p, s, with_codes(turned, code, t, edge + 1))
+        ready(p)
 
 
 def expand(values_ref, lead, slots, pad, count, out_ref, base):
@@ -164,11 +165,6 @@
     def put_right(t, p, slot, block):
         right_own[t, p, slot] = block
 
-    loads[0].wait()
-    loads[1].wait()
-    lay_right(edge, right_values, right_codes, right_stack, right_spread, put_right)
-    pl.semaphore_wait(barrier, columns + rows - 2 + jnp.where(me > 0, 1, 0) + jnp.where(me < n - 1, 1, 0))
-
     paired = columns % 2 == 0
     partner = me_col + 1 - 2 * lax.rem(me_col, 2)
     strides = range(2, columns, 2) if paired else range(1, columns)
@@ -177,12 +173,12 @@
     def back(d):
         return lax.rem(me_col + columns - d, columns)
 
-    def tile_hop(other, origin):
+    def tile_hop(other, origin, p):
         return pltpu.make_async_remote_copy(
-            src_ref=right_own.at[other],
-            dst_ref=right_in.at[me_row, origin],
-            send_sem=tile_send.at[other],
-            recv_sem=tile_recv.at[origin],
+            src_ref=right_own.at[other, p],
+            dst_ref=right_in.at[me_row, origin, p],
+            send_sem=tile_send.at[other, p],
+            recv_sem=tile_recv.at[origin, p],
             device_id={"col": other},
             device_id_type=mesh_id,
         )
@@ -197,12 +193,12 @@
             device_id_type=mesh_id,
         )
 
-    def row_hop(e, slot, source):
+    def row_hop(e, slot, p, source):
         return pltpu.make_async_remote_copy(
             src_ref=source,
-            dst_ref=right_in.at[me_row, slot],
-            send_sem=row_send.at[e, slot],
-            recv_sem=row_recv.at[e, slot],
+            dst_ref=right_in.at[me_row, slot, p],
+            send_sem=row_send.at[e, slot, p],
+            recv_sem=row_recv.at[e, slot, p],
             device_id={"row": lax.rem(me_row + e, rows)},
             device_id_type=mesh_id,
         )
@@ -213,23 +209,33 @@
         hop.start()
         sent.append(hop)
 
-    def to_rows(slot, source):
+    def to_rows(slot, p, source):
         for e in range(1, rows):
-            go(row_hop(e, slot, source))
-
-    def pass_tile(slot):
-        tile_hop(slot, slot).wait_recv()
-        to_rows(slot, right_in.at[me_row, slot])
+            go(row_hop(e, slot, p, source))
+
+    def pass_tiles(slots):
+        for p in range(panels):
+            for slot in slots:
+                tile_hop(slot, slot, p).wait_recv()
+                to_rows(slot, p, right_in.at[me_row, slot, p])
 
     def wait_rows(slot):
         for e in range(1, rows):
-            row_hop(e, slot, right_in.at[me_row, slot]).wait_recv()
+            for p in range(panels):
+                row_hop(e, slot, p, right_in.at[me_row, slot, p]).wait_recv()
 
     near = [back(d) for d in strides]
     late = [lax.rem(partner + columns - d, columns) for d in strides] if paired else []
-    for slot in near + late + ([partner] if paired else []):
-        go(tile_hop(slot, me_col))
-    to_rows(me_col, right_own.at[me_col])
+    def send_tiles(p):
+        if p == 0:
+            pl.semaphore_wait(barrier, columns + rows - 2 + jnp.where(me > 0, 1, 0) + jnp.where(me < n - 1, 1, 0))
+        for slot in near + late + ([partner] if paired else []):
+            go(tile_hop(slot, me_col, p))
+        to_rows(me_col, p, right_own.at[me_col, p])
+
+    loads[0].wait()
+    loads[1].wait()
+    lay_right(edge, right_values, right_codes, right_stack, right_spread, put_right, send_tiles)
     loads[2].wait()
     loads[3].wait()
     lay_left(edge, left_values, left_codes, left_stack, left_spread, put_left)
@@ -322,12 +328,11 @@
     first = order(0)
     sums[first] = jnp.zeros(sums.shape[1:], jnp.float32)
     if paired:
-        pass_tile(partner)
+        pass_tiles([partner])
     each_panel(lambda p: fill_left(me_col, p))
     wait_rows(me_col)
     each_panel(lambda p: add_products(first, me_col * panels + p))
-    for slot in near + late:
-        pass_tile(slot)
+    pass_tiles(near + late)
     if paired:
         for p in range(panels):
             left_hop(partner, p, partner).wait_recv()
@@ -461,9 +466,8 @@
         ]
         + [travel] * 4
         + [dma((4,))]
-        + [dma((columns, panels))] * 2
-        + [dma((columns,))] * 2
-        + [dma((rows, columns))] * 2
+        + [dma((columns, panels))] * 4
+        + [dma((rows, columns, panels))] * 2
         + [dma((n - 1, pieces))] * 4,
         compiler_params=pltpu.CompilerParams(collective_id=0, has_side_effects=True, vmem_limit_bytes=56 << 20),
     )(*operands)

time: 59.9 us -> 59.5 us (level)
  no operation moved by 1% of the time
where the time goes in v6:
time: 59.5 us; the launch traced here: 59.4 us
  Pallas kernels  57.6 us (97%)
  local copies, waits for them, and re-layouts  1.79 us (3%)
    pallas_call x1, Pallas kernels, body(): pl.pallas_call(functools.partial(kernel, columns, rows, n, edge, piece),...  57.6 us
    unnamed x1, local copies, waits for them, and re-layouts  1.79 us

profile of v6, /device:TPU:8, one launch (start us, length us, event | category | flops | bytes accessed | tf_op | source)
XLA Modules:
  0.0 59.4 jit_solution(2845783372576784763)
XLA Ops:
  0.0 57.6 %shard_map.46 = bf16[184,1104]{1,0:T(8,128)(2,1)} custom-call(bf16[48,2,4,529]{3,2,1,0:T(4,128)(2,1)} %left_hbm.1, s32[2,4,48]{2,1,0:T(4,128)} %bitcast.7, bf16[2,20,3,4,529]{4,3,2,1,0:T(4,128)(2,1)} %bitcast.5, s32[2,3,4,20]{3,2,1,0:T(4,128)} %bitcast.6), custom_call_target="tpu_custom_call" | custom-call | tf_op jit(solution)/shard_map/pallas_call | solution.py:449
  57.6 1.8 %copy.6 = bf16[1104,184]{0,1:T(8,128)(2,1)} copy(bf16[1104,184]{0,1:T(8,128)(2,1)} %bitcast.4) | data formatting | bytes 812544
